TPU v7x, 32 devices: a whole 2x2x4 slice. The times are simulated.
32 devices in a mesh: slab: 8 (over z, y), plane: 4 (over x, core).
Axes of the slice: x: 2, y: 2, z: 4, core: 2. Of those that a mesh axis runs over, the one named last changes fastest.
Arguments:
- tissue_v: float32 [32, 64, 128], P('slab', 'plane'), may hold values from -4 to 4
- tissue_gates: float32 [40, 32, 64, 128], P(None, 'slab', 'plane'), may hold values from 0 to 1
- tissue_diff: float32 [32, 64, 128], P('slab', 'plane'), may hold values from 0.2 to 1
- fibre_v: float32 [128, 2048], P('slab', 'plane'), may hold values from -4 to 4
- fibre_gates: float32 [40, 128, 2048], P(None, 'slab', 'plane'), may hold values from 0 to 1
- fibre_diff: float32 [128, 2048], P('slab', 'plane'), may hold values from 0.2 to 1
- gate_half: float32 [40], replicated, may hold values from -3 to 3
- gate_rate: float32 [40], replicated, may hold values from 0.5 to 20
- gate_cond: float32 [40], replicated, may hold values from 0.01 to 0.15
- gate_rev: float32 [40], replicated, may hold values from -2 to 2
- junc_cond: float32 [8], replicated, may hold values from 0.25 to 2
- junc_fibre: int32 [131072], P(('slab', 'plane')), may hold values from 0 to 15
- junc_fcell: int32 [131072], P(('slab', 'plane')), may hold values from 0 to 511
- junc_owner: int32 [131072, 1], P(('slab', 'plane')), may hold values from 0 to 31; in each aligned block of 4096 rows (0 to 4095, 4096 to 8191, ...) at most 256 rows name the same one
- junc_tcell: int32 [131072], P(('slab', 'plane')), may hold values from 0 to 8191
- junc_class: int32 [131072], P(('slab', 'plane')), may hold values from 0 to 7
Outputs:
- tissue_out: float32 [32, 64, 128], P('slab', 'plane')
- fibre_out: float32 [128, 2048], P('slab', 'plane')
Inputs may be any that keep to these rules, and one draw needn't show every extreme that they name: `junc_owner`: among the junctions held by one device, no tissue block is named by more than 256 of them, and some block is named by exactly 256. `junc_fibre`: A fibre of the slab group of the device that holds the junction. `junc_fcell`: A cell of the holding device's share of that fibre. `junc_tcell`: numbered over the owner's block in the order z, y, x with x fastest.
All inputs are finite; a program needn't handle non-finite values.
Results may differ from a plain program's by a relative error of at most 0.00005.
Values sent between devices are 32-bit elements; how exact they have to be, the bound alone decides.
A program may use at most 64 MiB of HBM per device.

v0:
```python
import jax
import jax.numpy as jnp
from jax import lax
from jax.sharding import PartitionSpec as P

STEPS = 14


time_step = 0.1
gate_slope = 2.0


def shift_pair(up, down, axis):
    count = lax.axis_size(axis)
    forward = [(i, i + 1) for i in range(count - 1)]
    backward = [(target, source) for source, target in forward]
    return lax.ppermute(up, axis, forward), lax.ppermute(down, axis, backward)


def membrane(voltage, gates, gate_half, gate_rate, gate_cond, gate_rev):
    gate_shape = (gates.shape[0],) + (1,) * (gates.ndim - 1)
    gate_signs = (
        jnp.where(jnp.arange(gates.shape[0], dtype=jnp.int32) % 2 == 0, 1.0, -1.0)
        .astype(jnp.float32)
        .reshape(gate_shape)
    )
    shifted = voltage[None] - gate_half.reshape(gate_shape)
    steady = jax.nn.sigmoid(gate_signs * gate_slope * shifted)
    decay_factor = jnp.exp(
        -time_step * gate_rate.reshape(gate_shape) * (1.0 + jax.nn.sigmoid(shifted))
    )
    renewed = steady + (gates - steady) * decay_factor
    driving = gate_cond.reshape(gate_shape) * (voltage[None] - gate_rev.reshape(gate_shape))
    return (renewed, jnp.sum(driving * renewed, axis=0))


def line_count(length, offset, total):
    places = offset + jnp.arange(length, dtype=jnp.int32)
    return (places > 0).astype(jnp.float32) + (places < total - 1).astype(jnp.float32)


def class_gain(classes, junc_cond):
    return jnp.sum(
        jnp.where(
            classes[:, None] == jnp.arange(junc_cond.shape[0], dtype=jnp.int32)[None, :],
            junc_cond[None, :],
            jnp.zeros((), jnp.float32),
        ),
        axis=1,
    )


def make_onehot(indices, count):
    return (indices[:, None] == jnp.arange(count, dtype=jnp.int32)[None, :]).astype(jnp.float32)


def split_two(values):
    high = lax.reduce_precision(values, 8, 7)
    low = lax.reduce_precision(values - high, 8, 7)
    return high, low


def pick_split(rows, cols, table):
    depth, width = table.shape
    high, low = split_two(table)
    stacked = jnp.concatenate([high, low], axis=0).astype(jnp.bfloat16)
    onehot = rows[:, None] == (jnp.arange(2 * depth, dtype=jnp.int32) % depth)[None, :]
    rows_read = jnp.dot(
        onehot.astype(jnp.bfloat16), stacked, preferred_element_type=jnp.float32
    )
    chosen = cols[:, None] == jnp.arange(width, dtype=jnp.int32)[None, :]
    return jnp.sum(jnp.where(chosen, rows_read, 0.0), axis=1)


def place_split(rows, cols, values, depth, width):
    high, low = split_two(values)
    lanes = jnp.arange(2 * width, dtype=jnp.int32)
    both = jnp.where((lanes < width)[None, :], high[:, None], low[:, None])
    weighted = jnp.where(cols[:, None] == (lanes % width)[None, :], both, 0.0)
    onehot = (rows[:, None] == jnp.arange(depth, dtype=jnp.int32)[None, :]).astype(jnp.bfloat16)
    halves = lax.dot_general(
        onehot,
        weighted.astype(jnp.bfloat16),
        (((0,), (0,)), ((), ())),
        preferred_element_type=jnp.float32,
    )
    return halves[:, :width] + halves[:, width:]


def running_rank(owner_onehot):
    total, kinds = owner_onehot.shape
    tall = 128
    blocks = owner_onehot.astype(jnp.bfloat16).reshape(total // tall, tall, kinds)
    lower = jnp.tril(jnp.ones((tall, tall), jnp.bfloat16))
    within = jnp.einsum("ij,bjo->bio", lower, blocks, preferred_element_type=jnp.float32)
    sums = within[:, -1, :]
    count = total // tall
    before = jnp.tril(jnp.ones((count, count), jnp.float32), -1)
    ahead = jnp.dot(before, sums, precision=lax.Precision.HIGHEST)
    ranks = jnp.sum((within + ahead[:, None, :]).reshape(total, kinds) * owner_onehot, axis=1)
    return jnp.round(ranks).astype(jnp.int32) - 1


def place_values(row_onehot, col_onehot, values):
    weighted = col_onehot * values[:, None]
    return lax.dot_general(
        row_onehot,
        weighted,
        (((0,), (0,)), ((), ())),
        precision=lax.Precision.HIGHEST,
        preferred_element_type=jnp.float32,
    )


def trade_both(paired):
    return lax.all_to_all(paired, ("slab", "plane"), split_axis=1, concat_axis=1, tiled=True)


def body(
    tissue_v,
    tissue_gates,
    tissue_diff,
    fibre_v,
    fibre_gates,
    fibre_diff,
    gate_half,
    gate_rate,
    gate_cond,
    gate_rev,
    junc_cond,
    junc_fibre,
    junc_fcell,
    junc_owner,
    junc_tcell,
    junc_class,
):
    slab_count = lax.axis_size("slab")
    plane_count = lax.axis_size("plane")
    devices = slab_count * plane_count
    layers_dev, rows_dev, cols_dev = tissue_v.shape
    fibre_rows, fibre_cols = fibre_v.shape
    junctions = junc_fibre.shape[0]
    capacity = 2 * junctions // devices
    tissue_count = (
        line_count(layers_dev, lax.axis_index("slab") * layers_dev, layers_dev * slab_count)[
            :, None, None
        ]
        + line_count(rows_dev, lax.axis_index("plane") * rows_dev, rows_dev * plane_count)[
            None, :, None
        ]
        + line_count(cols_dev, 0, cols_dev)[None, None, :]
    )
    fibre_count = line_count(
        fibre_cols, lax.axis_index("plane") * fibre_cols, fibre_cols * plane_count
    )[None, :]
    fibre_cells = fibre_rows * fibre_cols
    fibre_width = 128
    fibre_grid_rows = fibre_cells // fibre_width
    tissue_grid_rows = layers_dev * rows_dev
    owners = junc_owner[:, 0]
    owner_onehot = make_onehot(owners, devices)
    rank_onehot = make_onehot(running_rank(owner_onehot), capacity)
    kinds = junc_cond.shape[0] + 1
    code = (junc_tcell * kinds + junc_class + 1).astype(jnp.float32)
    code_table = jnp.round(place_values(owner_onehot, rank_onehot, code)).astype(jnp.int32)
    fibre_index = (junc_fibre * fibre_cols + junc_fcell).astype(jnp.float32)
    fibre_table = jnp.round(place_values(owner_onehot, rank_onehot, fibre_index))
    own_cells = fibre_table.astype(jnp.int32).reshape(-1)
    sent_tables = jnp.stack([code_table // kinds, code_table % kinds - 1])
    got_tables = lax.all_to_all(
        sent_tables, ("slab", "plane"), split_axis=1, concat_axis=1, tiled=True
    )
    remote_cells = got_tables[0].reshape(-1)
    remote_gain = class_gain(got_tables[1].reshape(-1), junc_cond)
    own_gain = class_gain(sent_tables[1].reshape(-1), junc_cond)
    fibre_at_row, fibre_at_col = own_cells // fibre_width, own_cells % fibre_width
    cell_row, cell_col = remote_cells // cols_dev, remote_cells % cols_dev

    def advance(step_index, carry):
        tissue_now, tissue_state, fibre_now, fibre_state = carry
        fibre_grid = fibre_now.reshape(fibre_grid_rows, fibre_width)
        tissue_grid = tissue_now.reshape(tissue_grid_rows, cols_dev)
        end_pad = (0, cols_dev - fibre_rows)
        up = jnp.concatenate([tissue_now[:, -1], jnp.pad(fibre_now[:, -1], end_pad)[None]])
        down = jnp.concatenate([tissue_now[:, 0], jnp.pad(fibre_now[:, 0], end_pad)[None]])
        y_low, y_high = shift_pair(up, down, "plane")
        z_low, z_high = shift_pair(tissue_now[-1:], tissue_now[:1], "slab")
        fibre_at_slot = pick_split(fibre_at_row, fibre_at_col, fibre_grid)
        tissue_at_slot = pick_split(cell_row, cell_col, tissue_grid)
        paired = jnp.stack([fibre_at_slot, tissue_at_slot]).reshape(2, devices, capacity)
        traded = trade_both(paired).reshape(2, -1)
        current = remote_gain * (traded[0] - tissue_at_slot)
        fibre_current = own_gain * (fibre_at_slot - traded[1])
        tissue_source = place_split(
            cell_row, cell_col, current, tissue_grid_rows, cols_dev
        ).reshape(tissue_now.shape)
        fibre_source = place_split(
            fibre_at_row, fibre_at_col, fibre_current, fibre_grid_rows, fibre_width
        ).reshape(fibre_now.shape)
        sides = jnp.pad(tissue_now, ((0, 0), (0, 0), (1, 1)))
        neighbours = (
            jnp.concatenate([tissue_now[1:], z_high], axis=0)
            + jnp.concatenate([z_low, tissue_now[:-1]], axis=0)
            + jnp.concatenate([tissue_now[:, 1:], y_high[:-1, None]], axis=1)
            + jnp.concatenate([y_low[:-1, None], tissue_now[:, :-1]], axis=1)
            + sides[:, :, 2:]
            + sides[:, :, :-2]
        )
        tissue_lap = neighbours - tissue_count * tissue_now
        fibre_lap = (
            jnp.concatenate([fibre_now[:, 1:], y_high[-1, :fibre_rows, None]], axis=1)
            + jnp.concatenate([y_low[-1, :fibre_rows, None], fibre_now[:, :-1]], axis=1)
            - fibre_count * fibre_now
        )
        tissue_state, tissue_ionic = membrane(
            tissue_now, tissue_state, gate_half, gate_rate, gate_cond, gate_rev
        )
        fibre_state, fibre_ionic = membrane(
            fibre_now, fibre_state, gate_half, gate_rate, gate_cond, gate_rev
        )
        tissue_next = tissue_now + time_step * (
            tissue_diff * tissue_lap - tissue_ionic + tissue_source
        )
        fibre_next = fibre_now + time_step * (fibre_diff * fibre_lap - fibre_ionic - fibre_source)
        return (tissue_next, tissue_state, fibre_next, fibre_state)

    final = lax.fori_loop(0, STEPS, advance, (tissue_v, tissue_gates, fibre_v, fibre_gates))
    return (final[0], final[2])


def solution(mesh):
    in_specs = (
        P("slab", "plane", None),
        P(None, "slab", "plane", None),
        P("slab", "plane", None),
        P("slab", "plane"),
        P(None, "slab", "plane"),
        P("slab", "plane"),
        P(),
        P(),
        P(),
        P(),
        P(),
        P(("slab", "plane")),
        P(("slab", "plane")),
        P(("slab", "plane"), None),
        P(("slab", "plane")),
        P(("slab", "plane")),
    )
    out_specs = (P("slab", "plane", None), P("slab", "plane"))
    return jax.shard_map(body, mesh=mesh, in_specs=in_specs, out_specs=out_specs, check_vma=False)
```

profile of v0, /device:TPU:0, one launch (start us, length us, event | category | flops | bytes accessed | tf_op | source)
XLA Modules:
  0.0 494.1 jit_solution(6374147802733579538)
XLA Ops:
  5.3 7.3 %all-to-all-start.1 = ((s32[2,32,256]{2,0,1:T(2,128)}), s32[2,32,256]{2,0,1:T(2,128)S(1)}, u32[]{:S(2)}, u32[]{:S(2)}) async-start(s32[2,32,256]{2,0,1:T(2,128)} %copy.60), calls=%async_computation.1 | async-start | bytes 131072 | tf_op jit(solution)/shard_map/all_to_all | solution.py:170
  14.7 5.3 %all-to-all-done.1 = s32[2,32,256]{2,0,1:T(2,128)S(1)} async-done(((s32[2,32,256]{2,0,1:T(2,128)}), s32[2,32,256]{2,0,1:T(2,128)S(1)}, u32[]{:S(2)}, u32[]{:S(2)}) %all-to-all-start.1) | async-done | bytes 65568 | tf_op jit(solution)/shard_map/all_to_all | solution.py:170
  20.5 472.9 %while.20 = (s32[]{:T(128)}, f32[4,16,128]{2,1,0:T(8,128)S(1)}, f32[40,4,16,128]{3,2,1,0:T(8,128)S(1)}, f32[16,512]{1,0:T(8,128)S(1)}, f32[40,16,512]{2,1,0:T(8,...) while((s32[]{:T(128)}, f32[4,16,128]{2,1,0:T(8,128)S(1)}, ...), condition=%wide.region_8.9_spmd.clone, body=%wide.region_3.8_spmd.clone.sunk | while | flops 1107442944 | bytes 8335497 | solution.py:227
  22.0 4.5 collective-permute-start.1
  34.9 4.9 all-to-all-start
  42.5 4.6 all-to-all-done
  68.6 4.9 all-to-all-start
  76.3 4.6 all-to-all-done
  102.4 4.9 all-to-all-start
  110.0 4.6 all-to-all-done
  136.2 4.9 all-to-all-start
  143.8 4.6 all-to-all-done
  169.9 4.9 all-to-all-start
  177.6 4.6 all-to-all-done
  203.7 4.9 all-to-all-start
  211.3 4.6 all-to-all-done
  237.5 4.9 all-to-all-start
  245.1 4.6 all-to-all-done
  271.2 4.9 all-to-all-start
  278.9 4.6 all-to-all-done
  305.0 4.9 all-to-all-start
  312.6 4.6 all-to-all-done
  338.8 4.9 all-to-all-start
  346.4 4.6 all-to-all-done
  372.5 4.9 all-to-all-start
  380.2 4.6 all-to-all-done
  406.3 4.9 all-to-all-start
  413.9 4.6 all-to-all-done
  440.1 4.9 all-to-all-start
  447.7 4.6 all-to-all-done
  473.8 4.9 all-to-all-start
  481.5 4.6 all-to-all-done
  (826 shorter events, 337.6 us)
Async XLA Ops:
  20.7 33.6 %collective-permute-start = (f32[1,16,128]{2,1,0:T(8,128)S(1)}, f32[1,16,128]{2,1,0:T(8,128)S(1)}, u32[]{:S(2)}, u32[]{:S(2)}) collective-permute-start(f32[1,16,128]{2,1,0:T(8,128)S(1)} %get-tuple-element.600), channel_id=1, source_target_pairs={{4,0},{8,4},{12,8},{16,12},{20,16},{24,20},{28,24},{5,1},{9,5},{13... | collective-permute-start | bytes 24584 | tf_op jit(solution)/shard_map/while/body/eval_jaxpr/ppermute | solution.py:17
  22.0 32.3 %collective-permute-start.1 = (f32[1,16,128]{2,1,0:T(8,128)S(1)}, f32[1,16,128]{2,1,0:T(8,128)S(1)}, u32[]{:S(2)}, u32[]{:S(2)}) collective-permute-start(f32[1,16,128]{2,1,0:T(8,128)S(1)} %get-tuple-element.603), channel_id=1, source_target_pairs={{0,4},{4,8},{8,12},{12,16},{16,20},{20,24},{24,28},{1,5},{5,9},{9,... | collective-permute-start | bytes 24584 | tf_op jit(solution)/shard_map/while/body/eval_jaxpr/ppermute | solution.py:17
  26.8 15.5 %collective-permute-start.3 = (f32[5,128]{1,0:T(8,128)S(1)}, f32[5,128]{1,0:T(8,128)S(1)}, u32[]{:S(2)}, u32[]{:S(2)}) collective-permute-start(f32[5,128]{1,0:T(8,128)S(1)} %pad_maximum_fusion.8), channel_id=1, source_target_pairs={{0,1},{1,2},{2,3},{4,5},{5,6},{6,7},{8,9},{9,10},{10,11},{12,13},{... | collective-permute-start | bytes 7688 | tf_op jit(solution)/shard_map/while/body/eval_jaxpr/ppermute | solution.py:17
  54.5 33.6 %collective-permute-start = (f32[1,16,128]{2,1,0:T(8,128)S(1)}, f32[1,16,128]{2,1,0:T(8,128)S(1)}, u32[]{:S(2)}, u32[]{:S(2)}) collective-permute-start(f32[1,16,128]{2,1,0:T(8,128)S(1)} %get-tuple-element.600), channel_id=1, source_target_pairs={{4,0},{8,4},{12,8},{16,12},{20,16},{24,20},{28,24},{5,1},{9,5},{13... | collective-permute-start | bytes 24584 | tf_op jit(solution)/shard_map/while/body/eval_jaxpr/ppermute | solution.py:17
  55.8 32.3 %collective-permute-start.1 = (f32[1,16,128]{2,1,0:T(8,128)S(1)}, f32[1,16,128]{2,1,0:T(8,128)S(1)}, u32[]{:S(2)}, u32[]{:S(2)}) collective-permute-start(f32[1,16,128]{2,1,0:T(8,128)S(1)} %get-tuple-element.603), channel_id=1, source_target_pairs={{0,4},{4,8},{8,12},{12,16},{16,20},{20,24},{24,28},{1,5},{5,9},{9,... | collective-permute-start | bytes 24584 | tf_op jit(solution)/shard_map/while/body/eval_jaxpr/ppermute | solution.py:17
  60.6 15.5 %collective-permute-start.3 = (f32[5,128]{1,0:T(8,128)S(1)}, f32[5,128]{1,0:T(8,128)S(1)}, u32[]{:S(2)}, u32[]{:S(2)}) collective-permute-start(f32[5,128]{1,0:T(8,128)S(1)} %pad_maximum_fusion.8), channel_id=1, source_target_pairs={{0,1},{1,2},{2,3},{4,5},{5,6},{6,7},{8,9},{9,10},{10,11},{12,13},{... | collective-permute-start | bytes 7688 | tf_op jit(solution)/shard_map/while/body/eval_jaxpr/ppermute | solution.py:17
  88.2 33.6 %collective-permute-start = (f32[1,16,128]{2,1,0:T(8,128)S(1)}, f32[1,16,128]{2,1,0:T(8,128)S(1)}, u32[]{:S(2)}, u32[]{:S(2)}) collective-permute-start(f32[1,16,128]{2,1,0:T(8,128)S(1)} %get-tuple-element.600), channel_id=1, source_target_pairs={{4,0},{8,4},{12,8},{16,12},{20,16},{24,20},{28,24},{5,1},{9,5},{13... | collective-permute-start | bytes 24584 | tf_op jit(solution)/shard_map/while/body/eval_jaxpr/ppermute | solution.py:17
  89.5 32.3 %collective-permute-start.1 = (f32[1,16,128]{2,1,0:T(8,128)S(1)}, f32[1,16,128]{2,1,0:T(8,128)S(1)}, u32[]{:S(2)}, u32[]{:S(2)}) collective-permute-start(f32[1,16,128]{2,1,0:T(8,128)S(1)} %get-tuple-element.603), channel_id=1, source_target_pairs={{0,4},{4,8},{8,12},{12,16},{16,20},{20,24},{24,28},{1,5},{5,9},{9,... | collective-permute-start | bytes 24584 | tf_op jit(solution)/shard_map/while/body/eval_jaxpr/ppermute | solution.py:17
  94.3 15.5 %collective-permute-start.3 = (f32[5,128]{1,0:T(8,128)S(1)}, f32[5,128]{1,0:T(8,128)S(1)}, u32[]{:S(2)}, u32[]{:S(2)}) collective-permute-start(f32[5,128]{1,0:T(8,128)S(1)} %pad_maximum_fusion.8), channel_id=1, source_target_pairs={{0,1},{1,2},{2,3},{4,5},{5,6},{6,7},{8,9},{9,10},{10,11},{12,13},{... | collective-permute-start | bytes 7688 | tf_op jit(solution)/shard_map/while/body/eval_jaxpr/ppermute | solution.py:17
  122.0 33.6 %collective-permute-start = (f32[1,16,128]{2,1,0:T(8,128)S(1)}, f32[1,16,128]{2,1,0:T(8,128)S(1)}, u32[]{:S(2)}, u32[]{:S(2)}) collective-permute-start(f32[1,16,128]{2,1,0:T(8,128)S(1)} %get-tuple-element.600), channel_id=1, source_target_pairs={{4,0},{8,4},{12,8},{16,12},{20,16},{24,20},{28,24},{5,1},{9,5},{13... | collective-permute-start | bytes 24584 | tf_op jit(solution)/shard_map/while/body/eval_jaxpr/ppermute | solution.py:17
  123.3 32.3 %collective-permute-start.1 = (f32[1,16,128]{2,1,0:T(8,128)S(1)}, f32[1,16,128]{2,1,0:T(8,128)S(1)}, u32[]{:S(2)}, u32[]{:S(2)}) collective-permute-start(f32[1,16,128]{2,1,0:T(8,128)S(1)} %get-tuple-element.603), channel_id=1, source_target_pairs={{0,4},{4,8},{8,12},{12,16},{16,20},{20,24},{24,28},{1,5},{5,9},{9,... | collective-permute-start | bytes 24584 | tf_op jit(solution)/shard_map/while/body/eval_jaxpr/ppermute | solution.py:17
  128.1 15.5 %collective-permute-start.3 = (f32[5,128]{1,0:T(8,128)S(1)}, f32[5,128]{1,0:T(8,128)S(1)}, u32[]{:S(2)}, u32[]{:S(2)}) collective-permute-start(f32[5,128]{1,0:T(8,128)S(1)} %pad_maximum_fusion.8), channel_id=1, source_target_pairs={{0,1},{1,2},{2,3},{4,5},{5,6},{6,7},{8,9},{9,10},{10,11},{12,13},{... | collective-permute-start | bytes 7688 | tf_op jit(solution)/shard_map/while/body/eval_jaxpr/ppermute | solution.py:17
  155.8 33.6 %collective-permute-start = (f32[1,16,128]{2,1,0:T(8,128)S(1)}, f32[1,16,128]{2,1,0:T(8,128)S(1)}, u32[]{:S(2)}, u32[]{:S(2)}) collective-permute-start(f32[1,16,128]{2,1,0:T(8,128)S(1)} %get-tuple-element.600), channel_id=1, source_target_pairs={{4,0},{8,4},{12,8},{16,12},{20,16},{24,20},{28,24},{5,1},{9,5},{13... | collective-permute-start | bytes 24584 | tf_op jit(solution)/shard_map/while/body/eval_jaxpr/ppermute | solution.py:17
  157.1 32.3 %collective-permute-start.1 = (f32[1,16,128]{2,1,0:T(8,128)S(1)}, f32[1,16,128]{2,1,0:T(8,128)S(1)}, u32[]{:S(2)}, u32[]{:S(2)}) collective-permute-start(f32[1,16,128]{2,1,0:T(8,128)S(1)} %get-tuple-element.603), channel_id=1, source_target_pairs={{0,4},{4,8},{8,12},{12,16},{16,20},{20,24},{24,28},{1,5},{5,9},{9,... | collective-permute-start | bytes 24584 | tf_op jit(solution)/shard_map/while/body/eval_jaxpr/ppermute | solution.py:17
  189.5 33.6 %collective-permute-start = (f32[1,16,128]{2,1,0:T(8,128)S(1)}, f32[1,16,128]{2,1,0:T(8,128)S(1)}, u32[]{:S(2)}, u32[]{:S(2)}) collective-permute-start(f32[1,16,128]{2,1,0:T(8,128)S(1)} %get-tuple-element.600), channel_id=1, source_target_pairs={{4,0},{8,4},{12,8},{16,12},{20,16},{24,20},{28,24},{5,1},{9,5},{13... | collective-permute-start | bytes 24584 | tf_op jit(solution)/shard_map/while/body/eval_jaxpr/ppermute | solution.py:17
  190.8 32.3 %collective-permute-start.1 = (f32[1,16,128]{2,1,0:T(8,128)S(1)}, f32[1,16,128]{2,1,0:T(8,128)S(1)}, u32[]{:S(2)}, u32[]{:S(2)}) collective-permute-start(f32[1,16,128]{2,1,0:T(8,128)S(1)} %get-tuple-element.603), channel_id=1, source_target_pairs={{0,4},{4,8},{8,12},{12,16},{16,20},{20,24},{24,28},{1,5},{5,9},{9,... | collective-permute-start | bytes 24584 | tf_op jit(solution)/shard_map/while/body/eval_jaxpr/ppermute | solution.py:17
  223.3 33.6 %collective-permute-start = (f32[1,16,128]{2,1,0:T(8,128)S(1)}, f32[1,16,128]{2,1,0:T(8,128)S(1)}, u32[]{:S(2)}, u32[]{:S(2)}) collective-permute-start(f32[1,16,128]{2,1,0:T(8,128)S(1)} %get-tuple-element.600), channel_id=1, source_target_pairs={{4,0},{8,4},{12,8},{16,12},{20,16},{24,20},{28,24},{5,1},{9,5},{13... | collective-permute-start | bytes 24584 | tf_op jit(solution)/shard_map/while/body/eval_jaxpr/ppermute | solution.py:17
  224.6 32.3 %collective-permute-start.1 = (f32[1,16,128]{2,1,0:T(8,128)S(1)}, f32[1,16,128]{2,1,0:T(8,128)S(1)}, u32[]{:S(2)}, u32[]{:S(2)}) collective-permute-start(f32[1,16,128]{2,1,0:T(8,128)S(1)} %get-tuple-element.603), channel_id=1, source_target_pairs={{0,4},{4,8},{8,12},{12,16},{16,20},{20,24},{24,28},{1,5},{5,9},{9,... | collective-permute-start | bytes 24584 | tf_op jit(solution)/shard_map/while/body/eval_jaxpr/ppermute | solution.py:17
  257.1 33.6 %collective-permute-start = (f32[1,16,128]{2,1,0:T(8,128)S(1)}, f32[1,16,128]{2,1,0:T(8,128)S(1)}, u32[]{:S(2)}, u32[]{:S(2)}) collective-permute-start(f32[1,16,128]{2,1,0:T(8,128)S(1)} %get-tuple-element.600), channel_id=1, source_target_pairs={{4,0},{8,4},{12,8},{16,12},{20,16},{24,20},{28,24},{5,1},{9,5},{13... | collective-permute-start | bytes 24584 | tf_op jit(solution)/shard_map/while/body/eval_jaxpr/ppermute | solution.py:17
  258.4 32.3 %collective-permute-start.1 = (f32[1,16,128]{2,1,0:T(8,128)S(1)}, f32[1,16,128]{2,1,0:T(8,128)S(1)}, u32[]{:S(2)}, u32[]{:S(2)}) collective-permute-start(f32[1,16,128]{2,1,0:T(8,128)S(1)} %get-tuple-element.603), channel_id=1, source_target_pairs={{0,4},{4,8},{8,12},{12,16},{16,20},{20,24},{24,28},{1,5},{5,9},{9,... | collective-permute-start | bytes 24584 | tf_op jit(solution)/shard_map/while/body/eval_jaxpr/ppermute | solution.py:17
  290.8 33.6 %collective-permute-start = (f32[1,16,128]{2,1,0:T(8,128)S(1)}, f32[1,16,128]{2,1,0:T(8,128)S(1)}, u32[]{:S(2)}, u32[]{:S(2)}) collective-permute-start(f32[1,16,128]{2,1,0:T(8,128)S(1)} %get-tuple-element.600), channel_id=1, source_target_pairs={{4,0},{8,4},{12,8},{16,12},{20,16},{24,20},{28,24},{5,1},{9,5},{13... | collective-permute-start | bytes 24584 | tf_op jit(solution)/shard_map/while/body/eval_jaxpr/ppermute | solution.py:17
  292.1 32.3 %collective-permute-start.1 = (f32[1,16,128]{2,1,0:T(8,128)S(1)}, f32[1,16,128]{2,1,0:T(8,128)S(1)}, u32[]{:S(2)}, u32[]{:S(2)}) collective-permute-start(f32[1,16,128]{2,1,0:T(8,128)S(1)} %get-tuple-element.603), channel_id=1, source_target_pairs={{0,4},{4,8},{8,12},{12,16},{16,20},{20,24},{24,28},{1,5},{5,9},{9,... | collective-permute-start | bytes 24584 | tf_op jit(solution)/shard_map/while/body/eval_jaxpr/ppermute | solution.py:17
  324.6 33.6 %collective-permute-start = (f32[1,16,128]{2,1,0:T(8,128)S(1)}, f32[1,16,128]{2,1,0:T(8,128)S(1)}, u32[]{:S(2)}, u32[]{:S(2)}) collective-permute-start(f32[1,16,128]{2,1,0:T(8,128)S(1)} %get-tuple-element.600), channel_id=1, source_target_pairs={{4,0},{8,4},{12,8},{16,12},{20,16},{24,20},{28,24},{5,1},{9,5},{13... | collective-permute-start | bytes 24584 | tf_op jit(solution)/shard_map/while/body/eval_jaxpr/ppermute | solution.py:17
  325.9 32.3 %collective-permute-start.1 = (f32[1,16,128]{2,1,0:T(8,128)S(1)}, f32[1,16,128]{2,1,0:T(8,128)S(1)}, u32[]{:S(2)}, u32[]{:S(2)}) collective-permute-start(f32[1,16,128]{2,1,0:T(8,128)S(1)} %get-tuple-element.603), channel_id=1, source_target_pairs={{0,4},{4,8},{8,12},{12,16},{16,20},{20,24},{24,28},{1,5},{5,9},{9,... | collective-permute-start | bytes 24584 | tf_op jit(solution)/shard_map/while/body/eval_jaxpr/ppermute | solution.py:17
  358.4 33.6 %collective-permute-start = (f32[1,16,128]{2,1,0:T(8,128)S(1)}, f32[1,16,128]{2,1,0:T(8,128)S(1)}, u32[]{:S(2)}, u32[]{:S(2)}) collective-permute-start(f32[1,16,128]{2,1,0:T(8,128)S(1)} %get-tuple-element.600), channel_id=1, source_target_pairs={{4,0},{8,4},{12,8},{16,12},{20,16},{24,20},{28,24},{5,1},{9,5},{13... | collective-permute-start | bytes 24584 | tf_op jit(solution)/shard_map/while/body/eval_jaxpr/ppermute | solution.py:17
  359.7 32.3 %collective-permute-start.1 = (f32[1,16,128]{2,1,0:T(8,128)S(1)}, f32[1,16,128]{2,1,0:T(8,128)S(1)}, u32[]{:S(2)}, u32[]{:S(2)}) collective-permute-start(f32[1,16,128]{2,1,0:T(8,128)S(1)} %get-tuple-element.603), channel_id=1, source_target_pairs={{0,4},{4,8},{8,12},{12,16},{16,20},{20,24},{24,28},{1,5},{5,9},{9,... | collective-permute-start | bytes 24584 | tf_op jit(solution)/shard_map/while/body/eval_jaxpr/ppermute | solution.py:17
  392.1 33.6 %collective-permute-start = (f32[1,16,128]{2,1,0:T(8,128)S(1)}, f32[1,16,128]{2,1,0:T(8,128)S(1)}, u32[]{:S(2)}, u32[]{:S(2)}) collective-permute-start(f32[1,16,128]{2,1,0:T(8,128)S(1)} %get-tuple-element.600), channel_id=1, source_target_pairs={{4,0},{8,4},{12,8},{16,12},{20,16},{24,20},{28,24},{5,1},{9,5},{13... | collective-permute-start | bytes 24584 | tf_op jit(solution)/shard_map/while/body/eval_jaxpr/ppermute | solution.py:17
  393.4 32.3 %collective-permute-start.1 = (f32[1,16,128]{2,1,0:T(8,128)S(1)}, f32[1,16,128]{2,1,0:T(8,128)S(1)}, u32[]{:S(2)}, u32[]{:S(2)}) collective-permute-start(f32[1,16,128]{2,1,0:T(8,128)S(1)} %get-tuple-element.603), channel_id=1, source_target_pairs={{0,4},{4,8},{8,12},{12,16},{16,20},{20,24},{24,28},{1,5},{5,9},{9,... | collective-permute-start | bytes 24584 | tf_op jit(solution)/shard_map/while/body/eval_jaxpr/ppermute | solution.py:17
  425.9 33.6 %collective-permute-start = (f32[1,16,128]{2,1,0:T(8,128)S(1)}, f32[1,16,128]{2,1,0:T(8,128)S(1)}, u32[]{:S(2)}, u32[]{:S(2)}) collective-permute-start(f32[1,16,128]{2,1,0:T(8,128)S(1)} %get-tuple-element.600), channel_id=1, source_target_pairs={{4,0},{8,4},{12,8},{16,12},{20,16},{24,20},{28,24},{5,1},{9,5},{13... | collective-permute-start | bytes 24584 | tf_op jit(solution)/shard_map/while/body/eval_jaxpr/ppermute | solution.py:17
  427.2 32.3 %collective-permute-start.1 = (f32[1,16,128]{2,1,0:T(8,128)S(1)}, f32[1,16,128]{2,1,0:T(8,128)S(1)}, u32[]{:S(2)}, u32[]{:S(2)}) collective-permute-start(f32[1,16,128]{2,1,0:T(8,128)S(1)} %get-tuple-element.603), channel_id=1, source_target_pairs={{0,4},{4,8},{8,12},{12,16},{16,20},{20,24},{24,28},{1,5},{5,9},{9,... | collective-permute-start | bytes 24584 | tf_op jit(solution)/shard_map/while/body/eval_jaxpr/ppermute | solution.py:17
  459.7 33.6 %collective-permute-start = (f32[1,16,128]{2,1,0:T(8,128)S(1)}, f32[1,16,128]{2,1,0:T(8,128)S(1)}, u32[]{:S(2)}, u32[]{:S(2)}) collective-permute-start(f32[1,16,128]{2,1,0:T(8,128)S(1)} %get-tuple-element.600), channel_id=1, source_target_pairs={{4,0},{8,4},{12,8},{16,12},{20,16},{24,20},{28,24},{5,1},{9,5},{13... | collective-permute-start | bytes 24584 | tf_op jit(solution)/shard_map/while/body/eval_jaxpr/ppermute | solution.py:17
  461.0 32.3 %collective-permute-start.1 = (f32[1,16,128]{2,1,0:T(8,128)S(1)}, f32[1,16,128]{2,1,0:T(8,128)S(1)}, u32[]{:S(2)}, u32[]{:S(2)}) collective-permute-start(f32[1,16,128]{2,1,0:T(8,128)S(1)} %get-tuple-element.603), channel_id=1, source_target_pairs={{0,4},{4,8},{8,12},{12,16},{16,20},{20,24},{24,28},{1,5},{5,9},{9,... | collective-permute-start | bytes 24584 | tf_op jit(solution)/shard_map/while/body/eval_jaxpr/ppermute | solution.py:17
  (113 other events, 969.0 us)
where the time goes:
time: 496 us; the launch traced here: 494 us
  starting transfers between devices  196 us (40%)
  matrix products  164 us (33%)
  waiting for transfers between devices  70.3 us (14%)
  other arithmetic  47.9 us (10%)
  local copies, waits for them, and re-layouts  10.2 us (2%)
  loops' own time  5.33 us (1%)
    ppermute x56, starting transfers between devices, shift_pair(): return (lax.ppermute(up, axis, forward), lax.ppermute(down, axis, backward))  120 us
    dot_general x28, matrix products, place_split(): lax.dot_general(onehot, weighted.astype(jnp.bfloat16), (((0,), (0,)), (()...  96.1 us
    all_to_all x14, starting transfers between devices, trade_both(): lax.all_to_all(paired, ('slab', 'plane'), split_axis=1, concat_axis=1, ti...  68 us
    all_to_all x14, waiting for transfers between devices, trade_both(): lax.all_to_all(paired, ('slab', 'plane'), split_axis=1, concat_axis=1, ti...  64.9 us
    dot_general x28, matrix products, pick_split(): jnp.dot(onehot.astype(jnp.bfloat16), stacked, preferred_element_type=jnp....  63.1 us
    reduce_sum x28, other arithmetic, membrane(): return (renewed, jnp.sum(driving * renewed, axis=0))  33.5 us
  transfers between devices with their start and end apart: 71, of which 15 were waited for; matrix products, arithmetic and copies ran while one was open for 43% of the time, Pallas kernels for 0%

commit v1 on v0

v1 whole, which is shorter than its diff:
```python
import functools
import math

import jax
import jax.numpy as jnp
from jax import lax
from jax.experimental import pallas as pl
from jax.experimental.pallas import tpu as pltpu
from jax.sharding import PartitionSpec as P

STEPS = 14
MESH = pl.DeviceIdType.MESH

time_step = 0.1
LANES = 128
SUBS = 8
WAVES = 4
UNROLL = 4


def class_gain(classes, junc_cond):
    return jnp.sum(
        jnp.where(
            classes[..., None] == jnp.arange(junc_cond.shape[0], dtype=jnp.int32),
            junc_cond,
            jnp.zeros((), jnp.float32),
        ),
        axis=-1,
    )


def make_onehot(indices, count):
    return (indices[:, None] == jnp.arange(count, dtype=jnp.int32)[None, :]).astype(jnp.float32)


def running_rank(owner_onehot):
    total, kinds = owner_onehot.shape
    tall = 128
    blocks = owner_onehot.astype(jnp.bfloat16).reshape(total // tall, tall, kinds)
    lower = jnp.tril(jnp.ones((tall, tall), jnp.bfloat16))
    within = jnp.einsum("ij,bjo->bio", lower, blocks, preferred_element_type=jnp.float32)
    sums = within[:, -1, :]
    count = total // tall
    before = jnp.tril(jnp.ones((count, count), jnp.float32), -1)
    ahead = jnp.dot(before, sums, precision=lax.Precision.HIGHEST)
    ranks = jnp.sum((within + ahead[:, None, :]).reshape(total, kinds) * owner_onehot, axis=1)
    return jnp.round(ranks).astype(jnp.int32) - 1


def place_values(row_onehot, col_onehot, values):
    weighted = col_onehot * values[:, None]
    return lax.dot_general(
        row_onehot,
        weighted,
        (((0,), (0,)), ((), ())),
        precision=lax.Precision.HIGHEST,
        preferred_element_type=jnp.float32,
    )


def flip_bits(value, bits):
    out, place = value, 1
    while place <= bits:
        if bits & place:
            out = out + place * (1 - 2 * ((value // place) % 2))
        place *= 2
    return out


def lane_gather(source, index):
    return lax.gather(
        source,
        index[..., None],
        lax.GatherDimensionNumbers(
            offset_dims=(),
            collapsed_slice_dims=(1,),
            start_index_map=(1,),
            operand_batching_dims=(0,),
            start_indices_batching_dims=(0,),
        ),
        slice_sizes=(1, 1),
        mode=lax.GatherScatterMode.PROMISE_IN_BOUNDS,
    )


def steps_kernel(
    sizes,
    coef,
    tissue_v,
    tissue_gates,
    tissue_diff,
    fibre_v,
    fibre_gates,
    fibre_diff,
    grow,
    gcol,
    hotrow,
    gain,
    colhot,
    tissue_out,
    fibre_out,
    volt,
    gate,
    pre,
    diff,
    rowhot,
    send,
    local,
    recv,
    zrecv,
    hsend,
    hrecv,
    send_sem,
    recv_sem,
    hsend_sem,
    hrecv_sem,
):
    slabs, planes, layers, yb, fb, cb, deep = sizes
    n = slabs * planes
    nt = layers * yb
    nq = nt + fb * cb
    gates = gate.shape[0]
    rows = SUBS * nt
    chunk = 2 * deep
    per = SUBS // chunk
    groups = n // per
    wave = n // WAVES
    slab = lax.axis_index("slab")
    plane = lax.axis_index("plane")

    def device(k):
        return (flip_bits(slab, k // planes), flip_bits(plane, k % planes))

    barrier = pltpu.get_barrier_semaphore()
    zero = jnp.zeros((SUBS, LANES), jnp.float32)
    for par in range(2):
        for way in range(2):
            for i in range(yb):
                zrecv[par, way, i] = zero
            for i in range(fb + 1):
                hrecv[par, way, i] = zero
    for way in range(2):
        hsend[way, fb] = zero
    for k in range(1, n):
        pl.semaphore_signal(barrier, inc=1, device_id=device(k), device_id_type=MESH)

    for z in range(layers):
        for y in range(yb):
            volt[z * yb + y] = tissue_v[z, SUBS * y : SUBS * (y + 1), :]
            diff[z * yb + y] = time_step * tissue_diff[z, SUBS * y : SUBS * (y + 1), :]
    for f in range(fb):
        for c in range(cb):
            at = (slice(SUBS * f, SUBS * (f + 1)), slice(LANES * c, LANES * (c + 1)))
            volt[nt + f * cb + c] = fibre_v[at]
            diff[nt + f * cb + c] = time_step * fibre_diff[at]

    @pl.loop(0, gates)
    def _(k):
        sign = coef[5, k]
        for z in range(layers):
            for y in range(yb):
                old = tissue_gates[k, z, SUBS * y : SUBS * (y + 1), :]
                gate[k, z * yb + y] = (old + old - 1.0) * sign
        for f in range(fb):
            for c in range(cb):
                old = fibre_gates[k, SUBS * f : SUBS * (f + 1), LANES * c : LANES * (c + 1)]
                gate[k, nt + f * cb + c] = (old + old - 1.0) * sign

    places = lax.broadcasted_iota(jnp.int32, (rows, LANES), 0)

    @pl.loop(0, n)
    def _(k):
        for i in range(chunk):
            hot = places == jnp.broadcast_to(hotrow[k, i : i + 1, :], (rows, LANES))
            rowhot[k, i] = jnp.where(hot, 1.0, 0.0).astype(jnp.bfloat16)

    pl.semaphore_wait(barrier, n - 1)

    sub = lax.broadcasted_iota(jnp.int32, (SUBS, LANES), 0)
    lane = lax.broadcasted_iota(jnp.int32, (SUBS, LANES), 1)
    is_fibre = sub % chunk < deep

    def gather_group(m):
        row_at = grow[m]
        col_at = gcol[m]
        out = zero
        for r in range(rows):
            q, s = r // SUBS, r % SUBS
            source = jnp.where(
                is_fibre,
                jnp.broadcast_to(volt[nt + q, s : s + 1, :], (SUBS, LANES)),
                jnp.broadcast_to(volt[q, s : s + 1, :], (SUBS, LANES)),
            )
            out = jnp.where(row_at == r, lane_gather(source, col_at), out)
        return out

    def junction_copy(k, par):
        return pltpu.make_async_remote_copy(
            src_ref=send.at[k],
            dst_ref=recv.at[par, k],
            send_sem=send_sem,
            recv_sem=recv_sem.at[par, k // wave],
            device_id=device(k),
            device_id_type=MESH,
        )

    def z_copy(way, par):
        first = (layers - 1) * yb if way == 0 else 0
        return pltpu.make_async_remote_copy(
            src_ref=volt.at[pl.ds(first, yb)],
            dst_ref=zrecv.at[par, way],
            send_sem=hsend_sem.at[way],
            recv_sem=hrecv_sem.at[par, way],
            device_id=(slab + 1 - 2 * way, plane),
            device_id_type=MESH,
        )

    def h_copy(way, par):
        return pltpu.make_async_remote_copy(
            src_ref=hsend.at[way],
            dst_ref=hrecv.at[par, way],
            send_sem=hsend_sem.at[2 + way],
            recv_sem=hrecv_sem.at[par, 2 + way],
            device_id=(slab, plane + 1 - 2 * way),
            device_id_type=MESH,
        )

    halos = (
        (z_copy, 0, slab < slabs - 1, slab > 0),
        (z_copy, 1, slab > 0, slab < slabs - 1),
        (h_copy, 0, plane < planes - 1, plane > 0),
        (h_copy, 1, plane > 0, plane < planes - 1),
    )

    def flag(condition):
        return jnp.where(condition, 1.0, 0.0)

    @pl.loop(0, STEPS)
    def _(step):
        par = step % 2
        for m in range(groups - 1, -1, -1):
            got = gather_group(m)
            if chunk == SUBS:
                swapped = pltpu.roll(got, deep, 0)
            else:
                swapped = jnp.where(
                    is_fibre, pltpu.roll(got, SUBS - deep, 0), pltpu.roll(got, deep, 0)
                )
            for p in range(per):
                send[per * m + p] = got[chunk * p : chunk * (p + 1)]
                local[per * m + p] = swapped[chunk * p : chunk * (p + 1)]
            if m < groups - 1:
                for p in range(per - 1, -1, -1):
                    junction_copy(per * (m + 1) + p, par).start()
        recv[par, 0] = send[0]
        for f in range(fb):
            hsend[0, f] = pltpu.roll(volt[nt + f * cb + cb - 1], 1, 1)
            hsend[1, f] = pltpu.roll(volt[nt + f * cb], LANES - 1, 1)
        for z in range(layers):
            hsend[0, fb, z : z + 1, :] = volt[z * yb + yb - 1, SUBS - 1 : SUBS, :]
            hsend[1, fb, z : z + 1, :] = volt[z * yb, 0:1, :]
        for p in range(per - 1, 0, -1):
            junction_copy(p, par).start()
        for build, way, sends, receives in halos:

            @pl.when(sends)
            def _():
                build(way, par).start()

        half_set = nq // 2
        for first in (0, half_set):

            @functools.partial(
                lax.fori_loop, 0, gates // UNROLL, init_val=(zero,) * (2 * half_set)
            )
            def sums(step_k, carry):
                carry = list(carry)
                for u in range(UNROLL):
                    k = step_k * UNROLL + u
                    half, base, slope, cond, pull = (coef[i, k] for i in range(5))
                    for i in range(half_set):
                        q = first + i
                        shifted = volt[q] - half
                        target = jnp.tanh(shifted)
                        factor = jnp.exp2(base + slope * jnp.tanh(0.5 * shifted))
                        new = target + (gate[k, q] - target) * factor
                        gate[k, q] = new
                        carry[2 * i] = carry[2 * i] + cond * new
                        carry[2 * i + 1] = carry[2 * i + 1] + pull * new
                return tuple(carry)

            for i in range(half_set):
                pre[first + i] = volt[first + i] * (coef[6, 0] + sums[2 * i]) - (
                    coef[6, 1] + sums[2 * i + 1]
                )

        at_left, at_right = lane == 0, lane == LANES - 1
        for z in range(layers):
            for y in range(yb):
                q = z * yb + y
                v = volt[q]
                near = jnp.where(at_left, 0.0, pltpu.roll(v, 1, 1))
                near = near + jnp.where(at_right, 0.0, pltpu.roll(v, LANES - 1, 1))
                above = pltpu.roll(volt[q - 1], 1, 0) if y > 0 else zero
                below = pltpu.roll(volt[q + 1], SUBS - 1, 0) if y < yb - 1 else zero
                near = near + jnp.where(sub == 0, above, pltpu.roll(v, 1, 0))
                near = near + jnp.where(sub == SUBS - 1, below, pltpu.roll(v, SUBS - 1, 0))
                count = jnp.where(at_left | at_right, 5.0, 6.0)
                if y == 0:
                    count = count - jnp.where(sub == 0, flag(plane == 0), 0.0)
                if y == yb - 1:
                    count = count - jnp.where(sub == SUBS - 1, flag(plane == planes - 1), 0.0)
                if z > 0:
                    near = near + volt[q - yb]
                else:
                    count = count - flag(slab == 0)
                if z < layers - 1:
                    near = near + volt[q + yb]
                else:
                    count = count - flag(slab == slabs - 1)
                pre[q] = v + diff[q] * (near - count * v) - time_step * pre[q]
        for f in range(fb):
            for c in range(cb):
                q = nt + f * cb + c
                v = volt[q]
                before = pltpu.roll(volt[q - 1], 1, 1) if c > 0 else zero
                after = pltpu.roll(volt[q + 1], LANES - 1, 1) if c < cb - 1 else zero
                near = jnp.where(at_left, before, pltpu.roll(v, 1, 1))
                near = near + jnp.where(at_right, after, pltpu.roll(v, LANES - 1, 1))
                count = jnp.full((SUBS, LANES), 2.0, jnp.float32)
                if c == 0:
                    count = count - jnp.where(at_left, flag(plane == 0), 0.0)
                if c == cb - 1:
                    count = count - jnp.where(at_right, flag(plane == planes - 1), 0.0)
                pre[q] = v + diff[q] * (near - count * v) - time_step * pre[q]

        sums = [jnp.zeros((2 * rows, LANES), jnp.float32) for _ in range(2)]
        for w in range(WAVES):
            span = pl.ds(w * wave + (1 if w == 0 else 0), wave - (1 if w == 0 else 0))
            pltpu.make_async_copy(
                recv.at[par, span], recv.at[par, span], recv_sem.at[par, w]
            ).wait()
            for k in range(w * wave, (w + 1) * wave):
                flow = gain[k] * (recv[par, k] - local[k])
                for kind in range(2):
                    parts = []
                    for i in range(kind * deep, (kind + 1) * deep):
                        value = jnp.broadcast_to(flow[i : i + 1, :], (2 * SUBS, LANES))
                        high = value.astype(jnp.bfloat16)
                        low = (value - high.astype(jnp.float32)).astype(jnp.bfloat16)
                        hot = rowhot[k, i]
                        tall = rows // (2 * SUBS)
                        parts.append(
                            jnp.concatenate(
                                [hot * jnp.concatenate([high] * tall, axis=0)]
                                + [hot * jnp.concatenate([low] * tall, axis=0)],
                                axis=0,
                            )
                        )
                    wide = jnp.concatenate(parts, axis=1) if deep > 1 else parts[0]
                    sums[kind] = sums[kind] + jnp.dot(
                        wide, colhot[k, kind], preferred_element_type=jnp.float32
                    )
        pltpu.make_async_copy(send.at[pl.ds(1, n - 1)], send.at[pl.ds(1, n - 1)], send_sem).wait()
        for build, way, sends, receives in halos:

            @pl.when(receives)
            def _():
                build(way, par).wait_recv()

            @pl.when(sends)
            def _():
                build(way, par).wait_send()

        new = []
        for z in range(layers):
            for y in range(yb):
                q = z * yb + y
                source = sums[0][SUBS * q : SUBS * (q + 1)]
                source = source + sums[0][rows + SUBS * q : rows + SUBS * (q + 1)]
                halo = zero
                if z == 0:
                    halo = halo + zrecv[par, 0, y]
                if z == layers - 1:
                    halo = halo + zrecv[par, 1, y]
                if y == 0:
                    row = jnp.broadcast_to(hrecv[par, 0, fb, z : z + 1, :], (SUBS, LANES))
                    halo = halo + jnp.where(sub == 0, row, 0.0)
                if y == yb - 1:
                    row = jnp.broadcast_to(hrecv[par, 1, fb, z : z + 1, :], (SUBS, LANES))
                    halo = halo + jnp.where(sub == SUBS - 1, row, 0.0)
                new.append(pre[q] + diff[q] * halo + time_step * source)
        for f in range(fb):
            for c in range(cb):
                q = f * cb + c
                source = sums[1][SUBS * q : SUBS * (q + 1)]
                source = source + sums[1][rows + SUBS * q : rows + SUBS * (q + 1)]
                halo = zero
                if c == 0:
                    halo = halo + jnp.where(at_left, hrecv[par, 0, f], 0.0)
                if c == cb - 1:
                    halo = halo + jnp.where(at_right, hrecv[par, 1, f], 0.0)
                new.append(pre[nt + q] + diff[nt + q] * halo + time_step * source)
        for q in range(nq):
            volt[q] = new[q]

    for z in range(layers):
        for y in range(yb):
            tissue_out[z, SUBS * y : SUBS * (y + 1), :] = volt[z * yb + y]
    for f in range(fb):
        for c in range(cb):
            at = (slice(SUBS * f, SUBS * (f + 1)), slice(LANES * c, LANES * (c + 1)))
            fibre_out[at] = volt[nt + f * cb + c]


def body(
    tissue_v,
    tissue_gates,
    tissue_diff,
    fibre_v,
    fibre_gates,
    fibre_diff,
    gate_half,
    gate_rate,
    gate_cond,
    gate_rev,
    junc_cond,
    junc_fibre,
    junc_fcell,
    junc_owner,
    junc_tcell,
    junc_class,
):
    slabs = lax.axis_size("slab")
    planes = lax.axis_size("plane")
    n = slabs * planes
    me = lax.axis_index("slab") * planes + lax.axis_index("plane")
    layers, rows_dev, cols_dev = tissue_v.shape
    fibre_rows, fibre_cols = fibre_v.shape
    junctions = junc_fibre.shape[0]
    capacity = 2 * junctions // n
    deep = -(-capacity // LANES)
    chunk = 2 * deep
    yb, fb, cb = rows_dev // SUBS, fibre_rows // SUBS, fibre_cols // LANES
    nt = layers * yb
    nq = nt + fb * cb
    rows = nt * SUBS
    owner_onehot = make_onehot(junc_owner[:, 0], n)
    rank_onehot = make_onehot(running_rank(owner_onehot), capacity)
    kinds = junc_cond.shape[0] + 1
    code = (junc_tcell * kinds + junc_class + 1).astype(jnp.float32)
    code_table = jnp.round(place_values(owner_onehot, rank_onehot, code)).astype(jnp.int32)
    fibre_index = (junc_fibre * fibre_cols + junc_fcell).astype(jnp.float32)
    own_cells = jnp.round(place_values(owner_onehot, rank_onehot, fibre_index)).astype(jnp.int32)
    sent = jnp.stack([code_table // kinds, code_table % kinds - 1])
    got = lax.all_to_all(sent, ("slab", "plane"), split_axis=1, concat_axis=1, tiled=True)
    near = me ^ jnp.arange(n, dtype=jnp.int32)
    full = jnp.stack([own_cells, sent[1], got[0], got[1]])
    full = jnp.take(full, near, axis=1)
    edge = deep * LANES - capacity
    full = jnp.pad(full, ((0, 0), (0, 0), (0, edge)), constant_values=-1)
    full = full.reshape(4, n, deep, LANES)
    own, own_class, cell, cell_class = full[0], full[1], full[2], full[3]
    own, cell = jnp.maximum(own, 0), jnp.maximum(cell, 0)
    fibre, along = own // fibre_cols, own % fibre_cols
    own_row = ((fibre // SUBS) * cb + along // LANES) * SUBS + fibre % SUBS
    own_col = along % LANES
    cell_row, cell_col = cell // LANES, cell % LANES
    grow = jnp.concatenate([own_row, cell_row], axis=1).reshape(-1, SUBS, LANES)
    gcol = jnp.concatenate([own_col, cell_col], axis=1).reshape(-1, SUBS, LANES)
    hotrow = jnp.concatenate([cell_row, own_row], axis=1)
    gain = class_gain(jnp.concatenate([cell_class, own_class], axis=1), junc_cond)
    cols = jnp.stack([cell_col, own_col], axis=1).reshape(n, 2, deep * LANES)
    colhot = (cols[..., None] == jnp.arange(LANES, dtype=jnp.int32)).astype(jnp.bfloat16)
    sign = jnp.where(jnp.arange(gate_half.shape[0]) % 2 == 0, 1.0, -1.0).astype(jnp.float32)
    rate = (-time_step * math.log2(math.e)) * gate_rate
    half_cond = 0.5 * gate_cond
    total = jnp.zeros_like(gate_half).at[0].set(jnp.sum(half_cond))
    total = total.at[1].set(jnp.sum(half_cond * gate_rev))
    coef = jnp.stack(
        [
            gate_half,
            1.5 * rate,
            0.5 * rate,
            sign * half_cond,
            sign * half_cond * gate_rev,
            sign,
            total,
        ]
    )
    vmem = pl.BlockSpec(memory_space=pltpu.VMEM)
    return pl.pallas_call(
        functools.partial(steps_kernel, (slabs, planes, layers, yb, fb, cb, deep)),
        out_shape=(
            jax.ShapeDtypeStruct(tissue_v.shape, jnp.float32),
            jax.ShapeDtypeStruct(fibre_v.shape, jnp.float32),
        ),
        in_specs=[pl.BlockSpec(memory_space=pltpu.SMEM)] + [vmem] * 11,
        out_specs=(vmem, vmem),
        scratch_shapes=[
            pltpu.VMEM((nq, SUBS, LANES), jnp.float32),
            pltpu.VMEM((gate_half.shape[0], nq, SUBS, LANES), jnp.float32),
            pltpu.VMEM((nq, SUBS, LANES), jnp.float32),
            pltpu.VMEM((nq, SUBS, LANES), jnp.float32),
            pltpu.VMEM((n, chunk, rows, LANES), jnp.bfloat16),
            pltpu.VMEM((n, chunk, LANES), jnp.float32),
            pltpu.VMEM((n, chunk, LANES), jnp.float32),
            pltpu.VMEM((2, n, chunk, LANES), jnp.float32),
            pltpu.VMEM((2, 2, yb, SUBS, LANES), jnp.float32),
            pltpu.VMEM((2, fb + 1, SUBS, LANES), jnp.float32),
            pltpu.VMEM((2, 2, fb + 1, SUBS, LANES), jnp.float32),
            pltpu.SemaphoreType.DMA,
            pltpu.SemaphoreType.DMA((2, WAVES)),
            pltpu.SemaphoreType.DMA((4,)),
            pltpu.SemaphoreType.DMA((2, 4)),
        ],
        compiler_params=pltpu.CompilerParams(
            collective_id=0, has_side_effects=True, vmem_limit_bytes=58 * 1024 * 1024
        ),
    )(
        coef,
        tissue_v,
        tissue_gates,
        tissue_diff,
        fibre_v,
        fibre_gates,
        fibre_diff,
        grow,
        gcol,
        hotrow,
        gain,
        colhot,
    )


def solution(mesh):
    in_specs = (
        P("slab", "plane", None),
        P(None, "slab", "plane", None),
        P("slab", "plane", None),
        P("slab", "plane"),
        P(None, "slab", "plane"),
        P("slab", "plane"),
        P(),
        P(),
        P(),
        P(),
        P(),
        P(("slab", "plane")),
        P(("slab", "plane")),
        P(("slab", "plane"), None),
        P(("slab", "plane")),
        P(("slab", "plane")),
    )
    out_specs = (P("slab", "plane", None), P("slab", "plane"))
    return jax.shard_map(body, mesh=mesh, in_specs=in_specs, out_specs=out_specs, check_vma=False)
```

time: 496 us -> 135 us (0.27)
  starting transfers between devices: 196 us -> 7.33 us
  matrix products: 164 us -> 5.78 us
  Pallas kernels: 0 us -> 100 us
  waiting for transfers between devices: 70.3 us -> 2.59 us
  other arithmetic: 47.9 us -> 10.3 us
  loops' own time: 5.33 us -> 0 us
    dot_general x56 -> x0, matrix products: 159 us -> none  [the longest x28 96.1 us: place_split(): lax.dot_general(onehot, weighted.astype(jnp.bfloat16), (((0,), (0,)), (()...]
    ppermute x56 -> x0, starting transfers between devices: 120 us -> none  [shift_pair(): return (lax.ppermute(up, axis, forward), lax.ppermute(down, axis, backward))]
    pallas_call x0 -> x1, Pallas kernels: none -> 100 us  [body(): pl.pallas_call(functools.partial(steps_kernel, (slabs, planes, layers, yb...]
    all_to_all x15 -> x1, starting transfers between devices: 75.4 us -> 7.33 us  [body(): lax.all_to_all(sent, ('slab', 'plane'), split_axis=1, concat_axis=1, tile...]
    all_to_all x15 -> x1, waiting for transfers between devices: 70.2 us -> 2.59 us  [body(): lax.all_to_all(sent, ('slab', 'plane'), split_axis=1, concat_axis=1, tile...]
    reduce_sum x29 -> x2, other arithmetic: 33.7 us -> 1.49 us  [the longest x1 0.89 us: class_gain(): jnp.sum(jnp.where(classes[..., None] == jnp.arange(junc_cond.shape[0], dt...]
    another operation x43 -> x3, other arithmetic: 9.96 us -> 0.1 us  [the longest x1 0.09 us: body(): full = jnp.stack([own_cells, sent[1], got[0], got[1]])]
    another operation x1 -> x0, loops' own time: 5.33 us -> none  [body(): lax.fori_loop(0, STEPS, advance, (tissue_v, tissue_gates, fibre_v, fibre_...]
  transfers between devices with their start and end apart: 71 -> 1, of which waited for: 15 -> 1; matrix products, arithmetic and copies ran while one was open for 43% -> 3% of each run, Pallas kernels for 0% -> 0%
where the time goes in v1:
time: 135 us; the launch traced here: 134 us
  Pallas kernels  100 us (74%)
  other arithmetic  10.3 us (8%)
  starting transfers between devices  7.33 us (5%)
  local copies, waits for them, and re-layouts  6.59 us (5%)
  matrix products  5.78 us (4%)
  waiting for transfers between devices  2.59 us (2%)
    pallas_call x1, Pallas kernels, body(): pl.pallas_call(functools.partial(steps_kernel, (slabs, planes, layers, yb...  100 us
    all_to_all x1, starting transfers between devices, body(): lax.all_to_all(sent, ('slab', 'plane'), split_axis=1, concat_axis=1, tile...  7.33 us
    convert_element_type x1, other arithmetic, body(): (cols[..., None] == jnp.arange(LANES, dtype=jnp.int32)).astype(jnp.bfloat16)  4.96 us
    dot_general x2, matrix products, place_values(): lax.dot_general(row_onehot, weighted, (((0,), (0,)), ((), ())), precision...  4.62 us
    unnamed x18, local copies, waits for them, and re-layouts  2.79 us
  transfers between devices with their start and end apart: 1, of which 1 were waited for; matrix products, arithmetic and copies ran while one was open for 3% of the time, Pallas kernels for 0%

profile of v1, /device:TPU:0, one launch (start us, length us, event | category | flops | bytes accessed | tf_op | source)
XLA Modules:
  0.0 134.0 jit_solution(14550476331567527375)
XLA Ops:
  0.6 0.0 copy-start
  0.7 1.0 convolution_bitcast_fusion
  1.7 0.4 slice_reduce_fusion
  2.0 0.0 copy-start.4
  2.1 0.0 copy-start.5
  2.1 0.2 fusion.39
  2.3 1.0 select_reduce_fusion.1
  3.3 0.7 add_convert_fusion
  4.0 2.7 %fusion.32 = (s32[1,32,256]{2,1,0:T(8,128)S(1)}, s32[1,32,256]{2,1,0:T(8,128)S(1)}) fusion(f32[4096]{0:T(1024)S(1)} %add_convert_fusion, s32[4096]{0:T(1024)S(1)} %add_bitcast_fusion.1, s32[4096]{0:T(1024)} %bitcast.56), kind=kOutput, calls=%fused_computation.65 | convolution fusion | flops 405004288 | bytes 114688 | tf_op jit(solution)/shard_map/dot_general | solution.py:52
  6.7 0.7 copy.26
  7.4 7.3 %all-to-all-start = ((s32[2,32,256]{2,0,1:T(2,128)}), s32[2,32,256]{2,0,1:T(2,128)S(1)}, u32[]{:S(2)}, u32[]{:S(2)}) async-start(s32[2,32,256]{2,0,1:T(2,128)} %copy.26), calls=%async_computation | async-start | bytes 131072 | tf_op jit(solution)/shard_map/all_to_all | solution.py:456
  14.8 1.9 %fusion.17 = s32[1,32,256]{2,1,0:T(8,128)S(1)} fusion(f32[4096]{0:T(1024)S(1)} %add_convert_fusion.1, s32[4096]{0:T(1024)S(1)} %add_bitcast_fusion.1, s32[4096]{0:T(1024)S(1)} %bitcast.57), kind=kOutput, calls=%fused_computation.17 | convolution fusion | flops 404897792 | bytes 81920 | tf_op jit(solution)/shard_map/dot_general | solution.py:52
  16.8 0.6 multiply_reduce_fusion
  17.4 0.6 pad_bitcast_fusion
  18.2 0.8 scatter.9
  18.9 0.6 stack.52.coef
  19.5 2.6 %all-to-all-done = s32[2,32,256]{2,0,1:T(2,128)S(1)} async-done(((s32[2,32,256]{2,0,1:T(2,128)}), s32[2,32,256]{2,0,1:T(2,128)S(1)}, u32[]{:S(2)}, u32[]{:S(2)}) %all-to-all-start) | async-done | bytes 65568 | tf_op jit(solution)/shard_map/all_to_all | solution.py:456
  22.1 0.1 pad_add_fusion
  22.2 0.6 gather_fusion
  22.9 0.1 select_bitcast_fusion
  23.0 0.3 compare_reduce_fusion.1
  23.3 0.3 and_select_fusion.2
  23.5 0.2 fusion.56
  23.7 0.1 add_bitcast_fusion
  23.8 5.0 %fusion.colhot = bf16[32,2,256,128]{3,2,1,0:T(8,128)(2,1)} fusion(s32[32,2,256]{2,1,0:T(2,128)S(1)} %add_bitcast_fusion), kind=kLoop, calls=%fused_computation.2 | loop fusion | flops 4194304 | bytes 4259840 | tf_op jit(solution)/shard_map/convert_element_type | solution.py:474
  28.8 0.9 select_reduce_fusion.gain
  29.7 0.1 and_select_fusion.3
  29.8 0.3 and_select_fusion.4
  30.1 0.7 pad_add_fusion.4
  30.8 100.4 %shard_map.167 = (f32[4,16,128]{2,1,0:T(8,128)}, f32[16,512]{1,0:T(8,128)}) custom-call(f32[7,40]{1,0:T(8,128)} %stack.52.coef, f32[4,16,128]{2,1,0:T(8,128)} %tissue_v.1, f32[40,4,16,128]{3,2,1,0:T(8,128)} %tissue_gates.1, f32[4,16,128]{2,1,0:T(8,128)} %tissue_diff.1, f32[16,512]{1,0:T(8,128)} %fibre_v.1, f32[40,16,512]{2,1,0:T(8,128)} %fibre_gates.1, ...), custom_call_target="tpu_custom_call" | custom-call | tf_op jit(solution)/shard_map/pallas_call | solution.py:492
  131.3 1.4 %copy.32 = f32[4,16,128]{2,1,0:T(8,128)} copy(f32[4,16,128]{2,1,0:T(8,128)} %get-tuple-element.55) | data formatting | bytes 65536
  132.6 1.4 %copy.33 = f32[16,512]{1,0:T(8,128)} copy(f32[16,512]{1,0:T(8,128)} %get-tuple-element.56) | data formatting | bytes 65536
  (27 shorter events, 0.2 us)
Async XLA Ops:
  0.6 14.2 %copy-start = (s32[4096,1]{0,1:T(1,128)S(1)}, s32[4096,1]{0,1:T(1,128)}, u32[]{:S(2)}) copy-start(s32[4096,1]{0,1:T(1,128)} %param.33) | copy-start | bytes 49156
  0.6 14.1 %copy-start.7 = (f32[40]{0:T(128)S(1)}, f32[40]{0:T(128)}, u32[]{:S(2)}) copy-start(f32[40]{0:T(128)} %param.27) | copy-start | bytes 484
  0.7 14.1 %copy-start.1 = (s32[4096]{0:T(1024)S(1)}, s32[4096]{0:T(1024)}, u32[]{:S(2)}) copy-start(s32[4096]{0:T(1024)} %param.32) | copy-start | bytes 49156
  0.7 14.1 %copy-start.2 = (s32[4096]{0:T(1024)S(1)}, s32[4096]{0:T(1024)}, u32[]{:S(2)}) copy-start(s32[4096]{0:T(1024)} %param.31) | copy-start | bytes 49156
  2.0 14.7 %copy-start.4 = (f32[40]{0:T(128)S(1)}, f32[40]{0:T(128)}, u32[]{:S(2)}) copy-start(f32[40]{0:T(128)} %param.29) | copy-start | bytes 484
  2.1 14.7 %copy-start.5 = (f32[40]{0:T(128)S(1)}, f32[40]{0:T(128)}, u32[]{:S(2)}) copy-start(f32[40]{0:T(128)} %param.28) | copy-start | bytes 484
  2.3 16.6 %copy-start.6 = (f32[40]{0:T(128)S(1)}, f32[40]{0:T(128)}, u32[]{:S(2)}) copy-start(f32[40]{0:T(128)} %param.26) | copy-start | bytes 484
  7.4 14.7 %all-to-all-start = ((s32[2,32,256]{2,0,1:T(2,128)}), s32[2,32,256]{2,0,1:T(2,128)S(1)}, u32[]{:S(2)}, u32[]{:S(2)}) async-start(s32[2,32,256]{2,0,1:T(2,128)} %copy.26), calls=%async_computation | async-start | bytes 131072 | tf_op jit(solution)/shard_map/all_to_all | solution.py:456
  14.8 14.0 %copy-start.3 = (f32[8]{0:T(128)S(1)}, f32[8]{0:T(128)}, u32[]{:S(2)}) copy-start(f32[8]{0:T(128)} %param.30) | copy-start | bytes 100

commit v2 on v1

--- a/solution.py
+++ b/solution.py
@@ -16,46 +16,6 @@
 SUBS = 8
 WAVES = 4
 UNROLL = 4
-
-
-def class_gain(classes, junc_cond):
-    return jnp.sum(
-        jnp.where(
-            classes[..., None] == jnp.arange(junc_cond.shape[0], dtype=jnp.int32),
-            junc_cond,
-            jnp.zeros((), jnp.float32),
-        ),
-        axis=-1,
-    )
-
-
-def make_onehot(indices, count):
-    return (indices[:, None] == jnp.arange(count, dtype=jnp.int32)[None, :]).astype(jnp.float32)
-
-
-def running_rank(owner_onehot):
-    total, kinds = owner_onehot.shape
-    tall = 128
-    blocks = owner_onehot.astype(jnp.bfloat16).reshape(total // tall, tall, kinds)
-    lower = jnp.tril(jnp.ones((tall, tall), jnp.bfloat16))
-    within = jnp.einsum("ij,bjo->bio", lower, blocks, preferred_element_type=jnp.float32)
-    sums = within[:, -1, :]
-    count = total // tall
-    before = jnp.tril(jnp.ones((count, count), jnp.float32), -1)
-    ahead = jnp.dot(before, sums, precision=lax.Precision.HIGHEST)
-    ranks = jnp.sum((within + ahead[:, None, :]).reshape(total, kinds) * owner_onehot, axis=1)
-    return jnp.round(ranks).astype(jnp.int32) - 1
-
-
-def place_values(row_onehot, col_onehot, values):
-    weighted = col_onehot * values[:, None]
-    return lax.dot_general(
-        row_onehot,
-        weighted,
-        (((0,), (0,)), ((), ())),
-        precision=lax.Precision.HIGHEST,
-        preferred_element_type=jnp.float32,
-    )
 
 
 def flip_bits(value, bits):
@@ -67,53 +27,114 @@
     return out
 
 
-def lane_gather(source, index):
+def axis_gather(source, index, axis):
+    other = 1 - axis
     return lax.gather(
         source,
         index[..., None],
         lax.GatherDimensionNumbers(
             offset_dims=(),
-            collapsed_slice_dims=(1,),
-            start_index_map=(1,),
-            operand_batching_dims=(0,),
-            start_indices_batching_dims=(0,),
+            collapsed_slice_dims=(axis,),
+            start_index_map=(axis,),
+            operand_batching_dims=(other,),
+            start_indices_batching_dims=(other,),
         ),
         slice_sizes=(1, 1),
         mode=lax.GatherScatterMode.PROMISE_IN_BOUNDS,
     )
 
 
+def swap_partner(tiles, bit, sub_bits, lane_bits):
+    sub = lax.broadcasted_iota(jnp.int32, (SUBS, LANES), 0)
+    lane = lax.broadcasted_iota(jnp.int32, (SUBS, LANES), 1)
+    if bit < sub_bits:
+        return [tiles[v ^ (1 << bit)] for v in range(len(tiles))]
+    if bit < lane_bits:
+        axis, place, size, reach = 0, sub, SUBS, 1 << (bit - sub_bits)
+    else:
+        axis, place, size, reach = 1, lane, LANES, 1 << (bit - lane_bits)
+    if 2 * reach == size:
+        return [pltpu.roll(tile, reach, axis) for tile in tiles]
+    low = (place & reach) == 0
+    return [
+        jnp.where(low, pltpu.roll(tile, size - reach, axis), pltpu.roll(tile, reach, axis))
+        for tile in tiles
+    ]
+
+
+def sort_tiles(tiles):
+    sub = lax.broadcasted_iota(jnp.int32, (SUBS, LANES), 0)
+    lane = lax.broadcasted_iota(jnp.int32, (SUBS, LANES), 1)
+    sub_bits = (len(tiles) - 1).bit_length()
+    lane_bits = sub_bits + 3
+    bits = lane_bits + 7
+    spot = [v + (sub << sub_bits) + (lane << lane_bits) for v in range(len(tiles))]
+    for size in range(1, bits + 1):
+        for bit in range(size - 1, -1, -1):
+            others = swap_partner(tiles, bit, sub_bits, lane_bits)
+            new = []
+            for at, tile, other in zip(spot, tiles, others):
+                turn = (at >> bit) if size == bits else (at >> bit) ^ (at >> size)
+                new.append(
+                    jnp.where(
+                        (turn & 1) == 0, jnp.minimum(tile, other), jnp.maximum(tile, other)
+                    )
+                )
+            tiles = new
+    return tiles
+
+
 def steps_kernel(
     sizes,
-    coef,
+    half_ref,
+    rate_ref,
+    cond_ref,
+    rev_ref,
+    class_ref,
     tissue_v,
     tissue_gates,
     tissue_diff,
     fibre_v,
     fibre_gates,
     fibre_diff,
-    grow,
-    gcol,
-    hotrow,
-    gain,
-    colhot,
-    tissue_out,
-    fibre_out,
+    junc_owner,
+    junc_fibre,
+    junc_fcell,
+    junc_tcell,
+    junc_class,
+    out_ref,
     volt,
     gate,
     pre,
     diff,
     rowhot,
+    colhot,
     send,
     local,
     recv,
     zrecv,
     hsend,
     hrecv,
+    coef,
+    tissue_in,
+    fibre_in,
+    pad_a,
+    pad_b,
+    payload,
+    dense,
+    spread,
+    hotrow,
+    hotcol,
+    gain,
+    remote,
+    sent_codes,
+    got_codes,
     send_sem,
     recv_sem,
     hsend_sem,
     hrecv_sem,
+    gate_sem,
+    code_sems,
 ):
     slabs, planes, layers, yb, fb, cb, deep = sizes
     n = slabs * planes
@@ -122,7 +143,7 @@
     gates = gate.shape[0]
     rows = SUBS * nt
     chunk = 2 * deep
-    per = SUBS // chunk
+    per = SUBS // deep
     groups = n // per
     wave = n // WAVES
     slab = lax.axis_index("slab")
@@ -131,6 +152,12 @@
     def device(k):
         return (flip_bits(slab, k // planes), flip_bits(plane, k % planes))
 
+    loads = [
+        pltpu.make_async_copy(tissue_gates, tissue_in, gate_sem.at[0]),
+        pltpu.make_async_copy(fibre_gates, fibre_in, gate_sem.at[1]),
+    ]
+    for load in loads:
+        load.start()
     barrier = pltpu.get_barrier_semaphore()
     zero = jnp.zeros((SUBS, LANES), jnp.float32)
     for par in range(2):
@@ -154,44 +181,158 @@
             volt[nt + f * cb + c] = fibre_v[at]
             diff[nt + f * cb + c] = time_step * fibre_diff[at]
 
+    sub = lax.broadcasted_iota(jnp.int32, (SUBS, LANES), 0)
+    lane = lax.broadcasted_iota(jnp.int32, (SUBS, LANES), 1)
+    me = slab * planes + plane
+    classes = class_ref.shape[0]
+    codes = rows * LANES * classes
+    lines = junc_owner.shape[0]
+    blocks = lines // SUBS
+    total = lines * LANES
+    tiles = []
+    for v in range(blocks):
+        at = slice(SUBS * v, SUBS * (v + 1))
+        fibre, along = junc_fibre[at], junc_fcell[at]
+        row = (fibre // SUBS * cb + along // LANES) * SUBS + fibre % SUBS
+        code = junc_tcell[at] * classes + junc_class[at]
+        payload[at] = (row * LANES + along % LANES) * codes + code
+        tiles.append((junc_owner[at] ^ me) * total + (v * SUBS + sub) * LANES + lane)
+    tiles = sort_tiles(tiles)
+    for v in range(blocks):
+        pad_a[pl.ds(v, SUBS, stride=blocks), :] = tiles[v]
+    pad_b[:, 0:lines] = pad_a[...].T
+    fold = LANES // lines
+    lined = None
+    wide_lane = lax.broadcasted_iota(jnp.int32, (lines, LANES), 1)
+    for i in range(fold):
+        piece = pad_b[pl.ds(i, lines, stride=fold), :]
+        piece = pltpu.roll(piece, lines * i, 1) if i > 0 else piece
+        lined = piece if i == 0 else jnp.where(wide_lane >= lines * i, piece, lined)
+    facts = []
+    for v in range(blocks):
+        key = lined[SUBS * v : SUBS * (v + 1)]
+        spot = key % total
+        fact = jnp.zeros((SUBS, LANES), jnp.int32)
+        for r in range(lines):
+            line = jnp.broadcast_to(payload[r : r + 1, :], (SUBS, LANES))
+            fact = jnp.where(spot // LANES == r, axis_gather(line, spot % LANES, 1), fact)
+        dense[v, 0] = fact // codes // LANES
+        dense[v, 1] = fact // codes % LANES
+        facts.append((key // total, (v * SUBS + sub + 1) * (2 * codes) + fact % codes + 1))
+    for k in range(n):
+        found = jnp.zeros((SUBS, LANES), jnp.int32)
+        for owner, fact in facts:
+            found = found + jnp.where(owner == k, fact, 0)
+        reach = deep
+        while reach < SUBS:
+            found = found + pltpu.roll(found, reach, 0)
+            reach *= 2
+        sent_codes[k] = found[:deep] % (2 * codes)
+        spread[k] = jnp.maximum(found[:deep] // (2 * codes) - 1, 0)
+    got_codes[0] = sent_codes[0]
+
+    pl.semaphore_wait(barrier, n - 1)
+    for k in range(n - 1, 0, -1):
+        pltpu.make_async_remote_copy(
+            src_ref=sent_codes.at[k],
+            dst_ref=got_codes.at[k],
+            send_sem=code_sems.at[0],
+            recv_sem=code_sems.at[1],
+            device_id=device(k),
+            device_id_type=MESH,
+        ).start()
+
+    def set_coef(k, carry):
+        even = jnp.where(k % 2 == 0, 1.0, -1.0)
+        half_cond = 0.5 * cond_ref[k]
+        scaled = (-time_step * math.log2(math.e)) * rate_ref[k]
+        coef[0, k] = half_ref[k]
+        coef[1, k] = 1.5 * scaled
+        coef[2, k] = 0.5 * scaled
+        coef[3, k] = even * half_cond
+        coef[4, k] = even * half_cond * rev_ref[k]
+        coef[5, k] = even
+        return carry[0] + half_cond, carry[1] + half_cond * rev_ref[k]
+
+    zero_scalar = jnp.float32(0.0)
+    sum_cond, sum_pull = lax.fori_loop(0, gates, set_coef, (zero_scalar, zero_scalar))
+
+    places = lax.broadcasted_iota(jnp.int32, (rows, LANES), 0)
+    columns = lax.broadcasted_iota(jnp.int32, (LANES, LANES), 0)
+
+    def set_hot(k, kind, i, row, col):
+        hot = places == jnp.broadcast_to(row, (rows, LANES))
+        rowhot[k, kind * deep + i] = jnp.where(hot, 1.0, 0.0).astype(jnp.bfloat16)
+        hot = columns == jnp.broadcast_to(col, (LANES, LANES))
+        hot = jnp.where(hot, 1.0, 0.0).astype(jnp.bfloat16)
+        colhot[k, kind, LANES * i : LANES * (i + 1), :] = hot.T
+
+    def gain_of(code):
+        kind = code % classes
+        out = jnp.zeros(code.shape, jnp.float32)
+        for c in range(classes):
+            out = jnp.where(kind == c, class_ref[c], out)
+        return out
+
+    def tall_tile(value):
+        return jnp.concatenate([value] * (SUBS // deep), axis=0) if deep < SUBS else value
+
+    @pl.loop(0, n)
+    def _(k):
+        spot = tall_tile(spread[k])
+        row = jnp.zeros((SUBS, LANES), jnp.int32)
+        col = row
+        for v in range(blocks):
+            here = spot // SUBS == v
+            row = jnp.where(here, axis_gather(dense[v, 0], spot % SUBS, 0), row)
+            col = jnp.where(here, axis_gather(dense[v, 1], spot % SUBS, 0), col)
+        code = sent_codes[k]
+        gain[k, deep:chunk] = jnp.where(code > 0, gain_of(code - 1), 0.0)
+        for i in range(deep):
+            set_hot(k, 1, i, row[i : i + 1], col[i : i + 1])
+
+    for load in loads:
+        load.wait()
+
     @pl.loop(0, gates)
     def _(k):
         sign = coef[5, k]
         for z in range(layers):
             for y in range(yb):
-                old = tissue_gates[k, z, SUBS * y : SUBS * (y + 1), :]
+                old = tissue_in[k, z, SUBS * y : SUBS * (y + 1), :]
                 gate[k, z * yb + y] = (old + old - 1.0) * sign
         for f in range(fb):
             for c in range(cb):
-                old = fibre_gates[k, SUBS * f : SUBS * (f + 1), LANES * c : LANES * (c + 1)]
+                old = fibre_in[k, SUBS * f : SUBS * (f + 1), LANES * c : LANES * (c + 1)]
                 gate[k, nt + f * cb + c] = (old + old - 1.0) * sign
 
-    places = lax.broadcasted_iota(jnp.int32, (rows, LANES), 0)
+    far = pl.ds(1, n - 1)
+    pltpu.make_async_copy(got_codes.at[far], got_codes.at[far], code_sems.at[1]).wait()
+    pltpu.make_async_copy(sent_codes.at[far], sent_codes.at[far], code_sems.at[0]).wait()
 
     @pl.loop(0, n)
     def _(k):
-        for i in range(chunk):
-            hot = places == jnp.broadcast_to(hotrow[k, i : i + 1, :], (rows, LANES))
-            rowhot[k, i] = jnp.where(hot, 1.0, 0.0).astype(jnp.bfloat16)
-
-    pl.semaphore_wait(barrier, n - 1)
-
-    sub = lax.broadcasted_iota(jnp.int32, (SUBS, LANES), 0)
-    lane = lax.broadcasted_iota(jnp.int32, (SUBS, LANES), 1)
-    is_fibre = sub % chunk < deep
-
-    def gather_group(m):
-        row_at = grow[m]
-        col_at = gcol[m]
+        code = got_codes[k]
+        cell = jnp.maximum(code - 1, 0) // classes
+        gain[k, 0:deep] = jnp.where(code > 0, gain_of(code - 1), 0.0)
+        remote[0, k] = cell // LANES
+        remote[1, k] = cell % LANES
+        for i in range(deep):
+            set_hot(k, 0, i, cell[i : i + 1] // LANES, cell[i : i + 1] % LANES)
+
+    for m in range(n * deep // SUBS):
+        for kind in range(2):
+            parts = [remote[kind, m * (SUBS // deep) + p] for p in range(SUBS // deep)]
+            hotrow[kind, m] = jnp.concatenate(parts, axis=0) if len(parts) > 1 else parts[0]
+        parts = [spread[m * (SUBS // deep) + p] for p in range(SUBS // deep)]
+        hotcol[m] = jnp.concatenate(parts, axis=0) if len(parts) > 1 else parts[0]
+
+    def lookup(base, row_at, col_at):
         out = zero
         for r in range(rows):
-            q, s = r // SUBS, r % SUBS
-            source = jnp.where(
-                is_fibre,
-                jnp.broadcast_to(volt[nt + q, s : s + 1, :], (SUBS, LANES)),
-                jnp.broadcast_to(volt[q, s : s + 1, :], (SUBS, LANES)),
-            )
-            out = jnp.where(row_at == r, lane_gather(source, col_at), out)
+            line = volt[base + r // SUBS, r % SUBS : r % SUBS + 1, :]
+            line = jnp.broadcast_to(line, (SUBS, LANES))
+            out = jnp.where(row_at == r, axis_gather(line, col_at, 1), out)
         return out
 
     def junction_copy(k, par):
@@ -238,17 +379,22 @@
     @pl.loop(0, STEPS)
     def _(step):
         par = step % 2
+        own = [lookup(nt, dense[v, 0], dense[v, 1]) for v in range(blocks)]
         for m in range(groups - 1, -1, -1):
-            got = gather_group(m)
-            if chunk == SUBS:
-                swapped = pltpu.roll(got, deep, 0)
-            else:
-                swapped = jnp.where(
-                    is_fibre, pltpu.roll(got, SUBS - deep, 0), pltpu.roll(got, deep, 0)
+            tissue_part = lookup(0, hotrow[0, m], hotrow[1, m])
+            spot = hotcol[m]
+            fibre_part = zero
+            for v in range(blocks):
+                fibre_part = jnp.where(
+                    spot // SUBS == v, axis_gather(own[v], spot % SUBS, 0), fibre_part
                 )
             for p in range(per):
-                send[per * m + p] = got[chunk * p : chunk * (p + 1)]
-                local[per * m + p] = swapped[chunk * p : chunk * (p + 1)]
+                at = slice(deep * p, deep * (p + 1))
+                k = per * m + p
+                send[k, 0:deep] = fibre_part[at]
+                send[k, deep:chunk] = tissue_part[at]
+                local[k, 0:deep] = tissue_part[at]
+                local[k, deep:chunk] = fibre_part[at]
             if m < groups - 1:
                 for p in range(per - 1, -1, -1):
                     junction_copy(per * (m + 1) + p, par).start()
@@ -290,8 +436,8 @@
                 return tuple(carry)
 
             for i in range(half_set):
-                pre[first + i] = volt[first + i] * (coef[6, 0] + sums[2 * i]) - (
-                    coef[6, 1] + sums[2 * i + 1]
+                pre[first + i] = volt[first + i] * (sum_cond + sums[2 * i]) - (
+                    sum_pull + sums[2 * i + 1]
                 )
 
         at_left, at_right = lane == 0, lane == LANES - 1
@@ -340,9 +486,9 @@
             pltpu.make_async_copy(
                 recv.at[par, span], recv.at[par, span], recv_sem.at[par, w]
             ).wait()
-            for k in range(w * wave, (w + 1) * wave):
-                flow = gain[k] * (recv[par, k] - local[k])
-                for kind in range(2):
+            for kind in range(2):
+                for k in range(w * wave, (w + 1) * wave):
+                    flow = gain[k] * (recv[par, k] - local[k])
                     parts = []
                     for i in range(kind * deep, (kind + 1) * deep):
                         value = jnp.broadcast_to(flow[i : i + 1, :], (2 * SUBS, LANES))
@@ -352,8 +498,8 @@
                         tall = rows // (2 * SUBS)
                         parts.append(
                             jnp.concatenate(
-                                [hot * jnp.concatenate([high] * tall, axis=0)]
-                                + [hot * jnp.concatenate([low] * tall, axis=0)],
+                                [jnp.concatenate([high] * tall, axis=0) * hot]
+                                + [jnp.concatenate([low] * tall, axis=0) * hot],
                                 axis=0,
                             )
                         )
@@ -404,13 +550,7 @@
         for q in range(nq):
             volt[q] = new[q]
 
-    for z in range(layers):
-        for y in range(yb):
-            tissue_out[z, SUBS * y : SUBS * (y + 1), :] = volt[z * yb + y]
-    for f in range(fb):
-        for c in range(cb):
-            at = (slice(SUBS * f, SUBS * (f + 1)), slice(LANES * c, LANES * (c + 1)))
-            fibre_out[at] = volt[nt + f * cb + c]
+    out_ref[...] = volt[...]
 
 
 def body(
@@ -434,7 +574,6 @@
     slabs = lax.axis_size("slab")
     planes = lax.axis_size("plane")
     n = slabs * planes
-    me = lax.axis_index("slab") * planes + lax.axis_index("plane")
     layers, rows_dev, cols_dev = tissue_v.shape
     fibre_rows, fibre_cols = fibre_v.shape
     junctions = junc_fibre.shape[0]
@@ -445,92 +584,73 @@
     nt = layers * yb
     nq = nt + fb * cb
     rows = nt * SUBS
-    owner_onehot = make_onehot(junc_owner[:, 0], n)
-    rank_onehot = make_onehot(running_rank(owner_onehot), capacity)
-    kinds = junc_cond.shape[0] + 1
-    code = (junc_tcell * kinds + junc_class + 1).astype(jnp.float32)
-    code_table = jnp.round(place_values(owner_onehot, rank_onehot, code)).astype(jnp.int32)
-    fibre_index = (junc_fibre * fibre_cols + junc_fcell).astype(jnp.float32)
-    own_cells = jnp.round(place_values(owner_onehot, rank_onehot, fibre_index)).astype(jnp.int32)
-    sent = jnp.stack([code_table // kinds, code_table % kinds - 1])
-    got = lax.all_to_all(sent, ("slab", "plane"), split_axis=1, concat_axis=1, tiled=True)
-    near = me ^ jnp.arange(n, dtype=jnp.int32)
-    full = jnp.stack([own_cells, sent[1], got[0], got[1]])
-    full = jnp.take(full, near, axis=1)
-    edge = deep * LANES - capacity
-    full = jnp.pad(full, ((0, 0), (0, 0), (0, edge)), constant_values=-1)
-    full = full.reshape(4, n, deep, LANES)
-    own, own_class, cell, cell_class = full[0], full[1], full[2], full[3]
-    own, cell = jnp.maximum(own, 0), jnp.maximum(cell, 0)
-    fibre, along = own // fibre_cols, own % fibre_cols
-    own_row = ((fibre // SUBS) * cb + along // LANES) * SUBS + fibre % SUBS
-    own_col = along % LANES
-    cell_row, cell_col = cell // LANES, cell % LANES
-    grow = jnp.concatenate([own_row, cell_row], axis=1).reshape(-1, SUBS, LANES)
-    gcol = jnp.concatenate([own_col, cell_col], axis=1).reshape(-1, SUBS, LANES)
-    hotrow = jnp.concatenate([cell_row, own_row], axis=1)
-    gain = class_gain(jnp.concatenate([cell_class, own_class], axis=1), junc_cond)
-    cols = jnp.stack([cell_col, own_col], axis=1).reshape(n, 2, deep * LANES)
-    colhot = (cols[..., None] == jnp.arange(LANES, dtype=jnp.int32)).astype(jnp.bfloat16)
-    sign = jnp.where(jnp.arange(gate_half.shape[0]) % 2 == 0, 1.0, -1.0).astype(jnp.float32)
-    rate = (-time_step * math.log2(math.e)) * gate_rate
-    half_cond = 0.5 * gate_cond
-    total = jnp.zeros_like(gate_half).at[0].set(jnp.sum(half_cond))
-    total = total.at[1].set(jnp.sum(half_cond * gate_rev))
-    coef = jnp.stack(
-        [
-            gate_half,
-            1.5 * rate,
-            0.5 * rate,
-            sign * half_cond,
-            sign * half_cond * gate_rev,
-            sign,
-            total,
-        ]
-    )
+    lines = junctions // LANES
+    gates = gate_half.shape[0]
+    per = SUBS // deep
+    smem = pl.BlockSpec(memory_space=pltpu.SMEM)
+    hbm = pl.BlockSpec(memory_space=pl.ANY)
     vmem = pl.BlockSpec(memory_space=pltpu.VMEM)
-    return pl.pallas_call(
+    flat = [
+        x.reshape(lines, LANES) for x in (junc_owner, junc_fibre, junc_fcell, junc_tcell, junc_class)
+    ]
+    out = pl.pallas_call(
         functools.partial(steps_kernel, (slabs, planes, layers, yb, fb, cb, deep)),
-        out_shape=(
-            jax.ShapeDtypeStruct(tissue_v.shape, jnp.float32),
-            jax.ShapeDtypeStruct(fibre_v.shape, jnp.float32),
-        ),
-        in_specs=[pl.BlockSpec(memory_space=pltpu.SMEM)] + [vmem] * 11,
-        out_specs=(vmem, vmem),
+        out_shape=jax.ShapeDtypeStruct((nq, SUBS, LANES), jnp.float32),
+        in_specs=[smem] * 5 + [vmem, hbm, vmem, vmem, hbm, vmem] + [vmem] * 5,
+        out_specs=vmem,
         scratch_shapes=[
             pltpu.VMEM((nq, SUBS, LANES), jnp.float32),
-            pltpu.VMEM((gate_half.shape[0], nq, SUBS, LANES), jnp.float32),
+            pltpu.VMEM((gates, nq, SUBS, LANES), jnp.float32),
             pltpu.VMEM((nq, SUBS, LANES), jnp.float32),
             pltpu.VMEM((nq, SUBS, LANES), jnp.float32),
             pltpu.VMEM((n, chunk, rows, LANES), jnp.bfloat16),
+            pltpu.VMEM((n, 2, deep * LANES, LANES), jnp.bfloat16),
             pltpu.VMEM((n, chunk, LANES), jnp.float32),
             pltpu.VMEM((n, chunk, LANES), jnp.float32),
             pltpu.VMEM((2, n, chunk, LANES), jnp.float32),
             pltpu.VMEM((2, 2, yb, SUBS, LANES), jnp.float32),
             pltpu.VMEM((2, fb + 1, SUBS, LANES), jnp.float32),
             pltpu.VMEM((2, 2, fb + 1, SUBS, LANES), jnp.float32),
+            pltpu.SMEM((6, gates), jnp.float32),
+            pltpu.VMEM(tissue_gates.shape, jnp.float32),
+            pltpu.VMEM(fibre_gates.shape, jnp.float32),
+            pltpu.VMEM((lines, LANES), jnp.int32),
+            pltpu.VMEM((LANES, LANES), jnp.int32),
+            pltpu.VMEM((lines, LANES), jnp.int32),
+            pltpu.VMEM((lines // SUBS, 2, SUBS, LANES), jnp.int32),
+            pltpu.VMEM((n, deep, LANES), jnp.int32),
+            pltpu.VMEM((2, n // per, SUBS, LANES), jnp.int32),
+            pltpu.VMEM((n // per, SUBS, LANES), jnp.int32),
+            pltpu.VMEM((n, chunk, LANES), jnp.float32),
+            pltpu.VMEM((2, n, deep, LANES), jnp.int32),
+            pltpu.VMEM((n, deep, LANES), jnp.int32),
+            pltpu.VMEM((n, deep, LANES), jnp.int32),
             pltpu.SemaphoreType.DMA,
             pltpu.SemaphoreType.DMA((2, WAVES)),
             pltpu.SemaphoreType.DMA((4,)),
             pltpu.SemaphoreType.DMA((2, 4)),
+            pltpu.SemaphoreType.DMA((2,)),
+            pltpu.SemaphoreType.DMA((2,)),
         ],
         compiler_params=pltpu.CompilerParams(
             collective_id=0, has_side_effects=True, vmem_limit_bytes=58 * 1024 * 1024
         ),
     )(
-        coef,
+        gate_half,
+        gate_rate,
+        gate_cond,
+        gate_rev,
+        junc_cond,
         tissue_v,
         tissue_gates,
         tissue_diff,
         fibre_v,
         fibre_gates,
         fibre_diff,
-        grow,
-        gcol,
-        hotrow,
-        gain,
-        colhot,
+        *flat,
     )
+    fibre_out = out[nt:].reshape(fb, cb, SUBS, LANES).transpose(0, 2, 1, 3)
+    return out[:nt].reshape(tissue_v.shape), fibre_out.reshape(fibre_v.shape)
 
 
 def solution(mesh):

time: 135 us -> 105 us (0.78)
  other arithmetic: 10.3 us -> 0 us
  starting transfers between devices: 7.33 us -> 0 us
  matrix products: 5.78 us -> 0 us
  local copies, waits for them, and re-layouts: 6.59 us -> 1.4 us
  Pallas kernels: 100 us -> 103 us
  waiting for transfers between devices: 2.59 us -> 0 us
    all_to_all x1 -> x0, starting transfers between devices: 7.33 us -> none  [body(): lax.all_to_all(sent, ('slab', 'plane'), split_axis=1, concat_axis=1, tile...]
    dot_general x4 -> x0, matrix products: 5.78 us -> none  [the longest x2 4.62 us: place_values(): lax.dot_general(row_onehot, weighted, (((0,), (0,)), ((), ())), precision...]
    convert_element_type x3 -> x0, other arithmetic: 5.71 us -> none  [the longest x1 4.96 us: body(): (cols[..., None] == jnp.arange(LANES, dtype=jnp.int32)).astype(jnp.bfloat16)]
    unnamed x18 -> x0, local copies, waits for them, and re-layouts: 2.79 us -> none
    all_to_all x1 -> x0, waiting for transfers between devices: 2.59 us -> none  [body(): lax.all_to_all(sent, ('slab', 'plane'), split_axis=1, concat_axis=1, tile...]
    reduce_sum x3 -> x0, other arithmetic: 2.46 us -> none  [the longest x1 0.97 us: running_rank(): jnp.sum((within + ahead[:, None, :]).reshape(total, kinds) * owner_onehot...]
    pallas_call x1, Pallas kernels: 100 us -> 103 us  [body(): pl.pallas_call(functools.partial(steps_kernel, (slabs, planes, layers, yb...]
    another operation x5 -> x0, local copies, waits for them, and re-layouts: 2 us -> none  [the longest x2 1.26 us: body(): jnp.stack([gate_half, 1.5 * rate, 0.5 * rate, sign * half_cond, sign * ha...]
  transfers between devices with their start and end apart: 1 -> 0, of which waited for: 1 -> 0; matrix products, arithmetic and copies ran while one was open for 3% -> 0% of each run, Pallas kernels for 0% -> 0%
where the time goes in v2:
time: 105 us
  Pallas kernels  103 us (98%)
  local copies, waits for them, and re-layouts  1.4 us (1%)
    pallas_call x1, Pallas kernels, body(): pl.pallas_call(functools.partial(steps_kernel, (slabs, planes, layers, yb...  103 us

profile of v2, /device:TPU:0, one launch (start us, length us, event | category | flops | bytes accessed | tf_op | source)
XLA Modules:
  0.0 104.6 jit_solution(1230807586490723214)
XLA Ops:
  0.6 102.5 %shard_map.167 = f32[16,8,128]{2,1,0:T(8,128)} custom-call(f32[40]{0:T(128)} %half_ref.1, f32[40]{0:T(128)} %rate_ref.1, f32[40]{0:T(128)} %cond_ref.1, f32[40]{0:T(128)} %rev_ref.1, f32[8]{0:T(128)} %class_ref.1, f32[4,16,128]{2,1,0:T(8,128)} %tissue_v.1, f32[40,4,16,128]{3,2,1,0:T(8,128)} %tissue_gates.1, f32[4,16,128]{2,1,0:T(8,128)} %tissue_diff.1, ...), custom_call_target="tpu_custom_call" | custom-call | tf_op jit(solution)/shard_map/pallas_call | solution.py:596
  103.2 1.4 %fusion = (f32[8,8,128]{2,1,0:T(8,128)}, f32[8,8,128]{2,1,0:T(8,128)}) fusion(f32[16,8,128]{2,1,0:T(8,128)} %shard_map.167), kind=kLoop, calls=%fused_computation | loop fusion | bytes 131072 | tf_op jit(solution)/shard_map/slice | solution.py:652

commit v3 on v2

--- a/solution.py
+++ b/solution.py
@@ -265,7 +265,7 @@
         rowhot[k, kind * deep + i] = jnp.where(hot, 1.0, 0.0).astype(jnp.bfloat16)
         hot = columns == jnp.broadcast_to(col, (LANES, LANES))
         hot = jnp.where(hot, 1.0, 0.0).astype(jnp.bfloat16)
-        colhot[k, kind, LANES * i : LANES * (i + 1), :] = hot.T
+        colhot[k, kind, :, LANES * i : LANES * (i + 1)] = hot
 
     def gain_of(code):
         kind = code % classes
@@ -504,8 +504,11 @@
                             )
                         )
                     wide = jnp.concatenate(parts, axis=1) if deep > 1 else parts[0]
-                    sums[kind] = sums[kind] + jnp.dot(
-                        wide, colhot[k, kind], preferred_element_type=jnp.float32
+                    sums[kind] = sums[kind] + lax.dot_general(
+                        wide,
+                        colhot[k, kind],
+                        (((1,), (1,)), ((), ())),
+                        preferred_element_type=jnp.float32,
                     )
         pltpu.make_async_copy(send.at[pl.ds(1, n - 1)], send.at[pl.ds(1, n - 1)], send_sem).wait()
         for build, way, sends, receives in halos:
@@ -604,7 +607,7 @@
             pltpu.VMEM((nq, SUBS, LANES), jnp.float32),
             pltpu.VMEM((nq, SUBS, LANES), jnp.float32),
             pltpu.VMEM((n, chunk, rows, LANES), jnp.bfloat16),
-            pltpu.VMEM((n, 2, deep * LANES, LANES), jnp.bfloat16),
+            pltpu.VMEM((n, 2, LANES, deep * LANES), jnp.bfloat16),
             pltpu.VMEM((n, chunk, LANES), jnp.float32),
             pltpu.VMEM((n, chunk, LANES), jnp.float32),
             pltpu.VMEM((2, n, chunk, LANES), jnp.float32),

time: 105 us -> 98.7 us (0.940)
  Pallas kernels: 103 us -> 96.4 us
    pallas_call x1, Pallas kernels: 103 us -> 96.4 us  [body(): pl.pallas_call(functools.partial(steps_kernel, (slabs, planes, layers, yb...]
where the time goes in v3:
time: 98.7 us; the launch traced here: 98.4 us
  Pallas kernels  96.4 us (98%)
  local copies, waits for them, and re-layouts  1.4 us (1%)
    pallas_call x1, Pallas kernels, body(): pl.pallas_call(functools.partial(steps_kernel, (slabs, planes, layers, yb...  96.4 us

profile of v3, /device:TPU:0, one launch (start us, length us, event | category | flops | bytes accessed | tf_op | source)
XLA Modules:
  0.0 98.4 jit_solution(6348609141692817500)
XLA Ops:
  0.6 96.4 %shard_map.167 = f32[16,8,128]{2,1,0:T(8,128)} custom-call(f32[40]{0:T(128)} %half_ref.1, f32[40]{0:T(128)} %rate_ref.1, f32[40]{0:T(128)} %cond_ref.1, f32[40]{0:T(128)} %rev_ref.1, f32[8]{0:T(128)} %class_ref.1, f32[4,16,128]{2,1,0:T(8,128)} %tissue_v.1, f32[40,4,16,128]{3,2,1,0:T(8,128)} %tissue_gates.1, f32[4,16,128]{2,1,0:T(8,128)} %tissue_diff.1, ...), custom_call_target="tpu_custom_call" | custom-call | tf_op jit(solution)/shard_map/pallas_call | solution.py:599
  97.0 1.4 %fusion = (f32[8,8,128]{2,1,0:T(8,128)}, f32[8,8,128]{2,1,0:T(8,128)}) fusion(f32[16,8,128]{2,1,0:T(8,128)} %shard_map.167), kind=kLoop, calls=%fused_computation | loop fusion | bytes 131072 | tf_op jit(solution)/shard_map/slice | solution.py:655
